TPU v7x, 128 devices: a whole 4x4x4 slice. The times are simulated.
128 devices in a mesh: shard: 16 (over x_hi, z, core), rep: 8 (over x_lo, y).
Axes of the slice: x: 4 (x_hi: 2, x_lo: 2; x = x_hi * 2 + x_lo), y: 4, z: 4, core: 2. Of those that a mesh axis runs over, the one named last changes fastest.
Arguments:
- tokens: bfloat16 [49152, 5120], P(('shard', 'rep')), may hold values from -700 to 700
- norm_gain: float32 [5120], replicated, may hold values from 0.1 to 1.9
- key_bias: float32 [1024], replicated, may hold values from -4 to 4
- key_weight: bfloat16 [8192, 1024], P('shard'), may hold values from -0.078125 to 0.078125
- cotangent: bfloat16 [49152, 1024], P(('shard', 'rep')), may hold values from -40 to 40
- block_slot: int32 [40], replicated, may hold values from 0 to 63, as said below
Outputs:
- projected: bfloat16 [49152, 1024], P(('shard', 'rep'))
- token_grad: bfloat16 [49152, 5120], P(('shard', 'rep'))
- weight_grad: float32 [8192, 1024], P('shard')
- gain_grad: float32 [5120], replicated
- bias_grad: float32 [1024], replicated
Inputs may be any that keep to these rules, and one draw needn't show every extreme that they name: Entries are distinct; block b lies on the device of shard with index block_slot[b] // 4, at its local slot block_slot[b] % 4; in every draw some device holds 4 blocks.
All inputs are finite; a program needn't handle non-finite values.
Results may differ from a plain program's by a relative error of at most 0.013.
Values may be sent and summed in bfloat16 or wider, within the bound.
A program may use at most 128 MiB of HBM per device.

v0:
```python
import jax
import jax.numpy as jnp
from jax import lax
from jax.sharding import PartitionSpec as P

BLK = 128


EPS = 1e-06


def normalize(tokens, norm_gain):
    values = tokens.astype(jnp.float32)
    inv_rms = lax.rsqrt(jnp.mean(values * values, axis=-1, keepdims=True) + EPS)
    normed = (values * inv_rms * norm_gain).astype(jnp.bfloat16)
    return (values, inv_rms, normed)


def token_backward(values, inv_rms, grad_normed, norm_gain):
    scaled = grad_normed * norm_gain
    inner = jnp.mean(scaled * values, axis=-1, keepdims=True)
    return (inv_rms * (scaled - values * inv_rms * inv_rms * inner)).astype(jnp.bfloat16)


def local(tokens, norm_gain, key_bias, key_weight, cotangent, block_slot):
    values, inv_rms, normed = normalize(tokens, norm_gain)
    row_count = tokens.shape[0]
    width = tokens.shape[1]
    local_rows = key_weight.shape[0]
    shard_count = lax.axis_size("shard")
    replicas = lax.axis_size("rep")
    slot_total = shard_count * local_rows // BLK
    block_count = width // BLK
    block_of_slot = (
        jnp.full((slot_total,), -1, jnp.int32)
        .at[block_slot]
        .set(jnp.arange(block_count, dtype=jnp.int32))
    )
    present = block_of_slot >= 0
    normed_blocks = normed.reshape(row_count, block_count, BLK)
    normed_slots = jnp.take(normed_blocks, jnp.maximum(block_of_slot, 0), axis=1)
    normed_slots = jnp.where(present[None, :, None], normed_slots, jnp.zeros((), jnp.bfloat16))
    normed_slots = normed_slots.reshape(row_count, slot_total * BLK)
    whole_weight = lax.all_gather(key_weight, "shard", axis=0, tiled=True)
    forward = jnp.dot(normed_slots, whole_weight, preferred_element_type=jnp.float32)
    grad_slots = lax.dot_general(
        cotangent, whole_weight, (((1,), (1,)), ((), ())), preferred_element_type=jnp.float32
    )
    projected = (forward + key_bias).astype(jnp.bfloat16)
    grad_normed = jnp.take(grad_slots.reshape(row_count, slot_total, BLK), block_slot, axis=1)
    grad_normed = grad_normed.reshape(row_count, width)
    token_grad = token_backward(values, inv_rms, grad_normed, norm_gain)
    grad_scale = float(row_count * shard_count * replicas) ** (-0.5)
    group_sum = lax.psum_scatter(
        (
            lax.dot_general(
                normed_slots,
                cotangent,
                (((0,), (0,)), ((), ())),
                preferred_element_type=jnp.float32,
            )
            * grad_scale
        ).astype(jnp.bfloat16),
        "shard",
        scatter_dimension=0,
        tiled=True,
    ).astype(jnp.float32)
    gain_part = jnp.sum(grad_normed * values * inv_rms, axis=0) * grad_scale
    bias_part = jnp.sum(cotangent.astype(jnp.float32), axis=0) * grad_scale
    gain_group, bias_group = lax.psum((gain_part, bias_part), "shard")
    weight_grad, gain_grad, bias_grad = lax.psum((group_sum, gain_group, bias_group), "rep")
    return (projected, token_grad, weight_grad, gain_grad, bias_grad)


def solution(mesh):
    return jax.shard_map(
        local,
        mesh=mesh,
        in_specs=(
            P(("shard", "rep"), None),
            P(),
            P(),
            P("shard", None),
            P(("shard", "rep"), None),
            P(),
        ),
        out_specs=(
            P(("shard", "rep"), None),
            P(("shard", "rep"), None),
            P("shard", None),
            P(),
            P(),
        ),
        check_vma=False,
    )
```

profile of v0, /device:TPU:0, one launch (start us, length us, event | category | flops | bytes accessed | tf_op | source)
XLA Modules:
  0.0 444.3 jit_solution(16748864164420286203)
XLA Ops:
  7.2 0.0 copy-start.6
  7.2 0.0 copy-start.3
  7.2 0.0 all-gather.2.cloned.1.call-start
  7.2 0.7 all-gather.2.cloned.1.call-update
  7.9 0.0 reduce-scatter.2.cloned.1.call-start
  8.0 6.3 %copy.12 = bf16[384,5120]{0,1:T(8,128)(2,1)} copy(bf16[384,5120]{1,0:T(8,128)(2,1)} %param.6) | data formatting | bytes 7864320 | tf_op args[0]
  14.2 0.0 copy-done.6
  14.3 0.7 scatter_custom_fusion
  15.0 3.0 fusion.7
  18.1 0.1 broadcast_bitcast_fusion.2
  18.1 0.1 broadcast_bitcast_fusion
  18.2 103.6 %all-gather.2.cloned.1.call-done = bf16[8192,1024]{1,0:T(8,128)(2,1)} async-done(((bf16[512,1024]{1,0:T(8,128)(2,1)}), bf16[8192,1024]{1,0:T(8,128)(2,1)}) %all-gather.2.cloned.1.call-update) | async-done | bytes 16777232 | tf_op jit(solution)/shard_map/all_gather | solution.py:44
  121.8 0.0 copy-done.3
  121.8 12.9 %convolution_bitcast_fusion = f32[48,64,8,128]{3,2,1,0:T(8,128)} fusion(bf16[384,1024]{1,0:T(8,128)(2,1)S(1)} %copy-done.3, bf16[8192,1024]{1,0:T(8,128)(2,1)} %all-gather.2.cloned.1.call-done), kind=kOutput, calls=%fused_computation.24 | convolution fusion | flops 6442450944 | bytes 30146560 | tf_op jit(solution)/shard_map/dot_general | solution.py:46
  134.7 10.8 %copy.20 = f32[48,64,8,128]{3,2,0,1:T(8,128)} copy(f32[48,64,8,128]{3,2,1,0:T(8,128)} %convolution_bitcast_fusion) | data formatting | bytes 25165824 | tf_op jit(solution)/shard_map/reshape | solution.py:50
  145.5 8.7 %gather_fusion.1 = f32[40,384,128]{2,1,0:T(8,128)} fusion(f32[384,64,128]{2,0,1:T(8,128)} %bitcast.34, s32[1024]{0:T(1024)S(1)} %pad_clamp_fusion), kind=kCustom, calls=%fused_computation.1 | custom fusion | bytes 15728800 | tf_op jit(solution)/shard_map/jit(_take)/gather | solution.py:50
  154.3 0.0 copy-start.4
  154.3 9.1 %copy.16 = f32[384,40,128]{0,2,1:T(8,128)} copy(f32[384,40,128]{2,0,1:T(8,128)} %bitcast.35) | data formatting | bytes 15728640 | tf_op jit(solution)/shard_map/jit(_take)/gather | solution.py:50
  163.3 0.0 copy-done.4
  163.3 0.0 copy-start
  163.3 0.0 copy-start.1
  163.3 8.8 %fusion.10 = (f32[5120]{0:T(1024)S(1)}, f32[384]{0:T(512)S(1)}) fusion(bf16[384,5120]{0,1:T(8,128)(2,1)} %copy.12, f32[384,40,128]{0,2,1:T(8,128)} %copy.16, f32[384]{0:T(512)S(1)} %add_rsqrt_fusion, pred[5120]{0:T(1024)(128)(4,1)S(1)} %broadcast_bitcast_fusion.2, f32[5120]{0:T(1024)S(1)} %copy-done.4), kind=kLoop, calls=%fused_computation.19 | loop fusion | flops 15723136 | bytes 11845632 | tf_op jit(solution)/shard_map/reduce_sum | solution.py:68
  172.2 0.0 copy-done
  172.2 0.0 copy-done.1
  172.2 5.6 %fusion.6 = (bf16[384,5120]{0,1:T(8,128)(2,1)}, bf16[384,5120]{0,1:T(8,128)(2,1)}) fusion(bf16[384,5120]{0,1:T(8,128)(2,1)S(1)} %copy-done.1, f32[384,40,128]{0,2,1:T(8,128)S(1)} %copy-done, f32[384]{0:T(512)S(1)} %broadcast_multiply_fusion.2, f32[5120]{0:T(1024)S(1)} %copy-done.4, f32[384]{0:T(512)S(1)} %add_rsqrt_fusion, ...), kind=kLoop, calls=%fused_computation.15 | loop fusion | flops 21626880 | bytes 19689472 | tf_op jit(solution)/shard_map/convert_element_type | solution.py:22
  177.8 6.3 %copy.13 = bf16[384,40,128]{2,0,1:T(8,128)(2,1)} copy(bf16[384,40,128]{0,2,1:T(8,128)(2,1)} %bitcast.37) | data formatting | bytes 7864320 | tf_op jit(solution)/shard_map/reshape | solution.py:40
  184.1 6.1 %gather_fusion = bf16[64,384,128]{2,1,0:T(8,128)(2,1)} fusion(bf16[384,40,128]{2,0,1:T(8,128)(2,1)} %copy.13, s32[1024]{0:T(1024)S(1)} %pad_clamp_fusion.1), kind=kCustom, calls=%fused_computation | custom fusion | bytes 12583168 | tf_op jit(solution)/shard_map/jit(_take)/gather | solution.py:41
  190.2 8.6 %copy.14 = bf16[384,64,128]{0,2,1:T(8,128)(2,1)} copy(bf16[384,64,128]{2,0,1:T(8,128)(2,1)} %bitcast.36) | data formatting | bytes 12582912 | tf_op jit(solution)/shard_map/jit(_take)/gather | solution.py:41
  198.8 6.9 %fusion.12 = bf16[384,8192]{0,1:T(8,128)(2,1)S(1)} fusion(bf16[384,64,128]{0,2,1:T(8,128)(2,1)} %copy.14, pred[8192]{0:T(1024)(128)(4,1)S(1)} %get-tuple-element.21, pred[8192]{0:T(1024)(128)(4,1)S(1)} %get-tuple-element.22), kind=kLoop, calls=%fused_computation.23 | loop fusion | flops 6291456 | bytes 12599296 | tf_op jit(solution)/shard_map/jit(_where)/select_n | solution.py:42
  205.8 0.0 copy-start.2
  205.8 2.6 copy-done.2
  208.3 11.7 %multiply_convert_fusion = bf16[8192,1024]{1,0:T(8,128)(2,1)} fusion(bf16[384,8192]{0,1:T(8,128)(2,1)S(1)} %fusion.12, bf16[384,1024]{1,0:T(8,128)(2,1)S(1)} %copy-done.3), kind=kOutput, calls=%fused_computation.3 | convolution fusion | flops 6459228160 | bytes 23855104 | tf_op jit(solution)/shard_map/dot_general | solution.py:56
  220.0 0.0 reduce-scatter.2.cloned.1.call-update
  220.0 0.0 copy-start.5
  220.0 0.1 convert_reduce_fusion
  220.2 6.3 %copy.17 = bf16[384,5120]{1,0:T(8,128)(2,1)} copy(bf16[384,5120]{0,1:T(8,128)(2,1)} %get-tuple-element.17) | data formatting | bytes 7864320
  226.5 66.6 %all-reduce = (f32[5120]{0:T(1024)S(1)}, f32[1024]{0:T(1024)S(1)}) all-reduce(f32[5120]{0:T(1024)S(1)} %broadcast_multiply_fusion, f32[1024]{0:T(1024)S(1)} %broadcast_multiply_fusion.1), channel_id=1, replica_groups=mesh['shard'=16,'rep'=8] {'shard'}, use_global_device_ids=true, to_apply=%region_6.7 | all-reduce | flops 6144 | bytes 49152 | tf_op jit(solution)/shard_map/psum | solution.py:70
  293.0 0.0 copy-done.5
  293.0 13.1 %add_convert_fusion = bf16[384,1024]{1,0:T(8,128)(2,1)} fusion(bf16[384,8192]{0,1:T(8,128)(2,1)} %copy-done.2, bf16[8192,1024]{1,0:T(8,128)(2,1)} %all-gather.2.cloned.1.call-done, f32[1024]{0:T(1024)S(1)} %copy-done.5), kind=kOutput, calls=%fused_computation.26 | convolution fusion | flops 6443237376 | bytes 23859200 | tf_op jit(solution)/shard_map/dot_general | solution.py:45
  306.1 59.4 %reduce-scatter.2.cloned.1.call-done = bf16[512,1024]{1,0:T(8,128)(2,1)} async-done(((bf16[8192,1024]{1,0:T(8,128)(2,1)}), bf16[512,1024]{1,0:T(8,128)(2,1)}) %reduce-scatter.2.cloned.1.call-update) | async-done | bytes 1048592 | tf_op jit(solution)/shard_map/reduce_scatter | solution.py:54
  365.5 71.9 %all-reduce.3 = (f32[512,1024]{1,0:T(8,128)}, f32[5120]{0:T(1024)}, f32[1024]{0:T(1024)}) all-reduce(bf16[512,1024]{1,0:T(8,128)(2,1)} %reduce-scatter.2.cloned.1.call-done, f32[5120]{0:T(1024)S(1)} %get-tuple-element.12, f32[1024]{0:T(1024)S(1)} %get-tuple-element.13), channel_id=1, replica_groups=mesh['shard'=16,'rep'=8] {'rep'}, use_global_device_ids=true, to_apply=%region_4.5 | all-reduce | flops 530432 | bytes 3194880 | tf_op jit(solution)/shard_map/psum | solution.py:71
  (11 shorter events, 0.1 us)
Async XLA Ops:
  7.2 7.1 %copy-start.6 = (s32[40]{0:T(128)S(1)}, s32[40]{0:T(128)}, u32[]{:S(2)}) copy-start(s32[40]{0:T(128)} %param.11) | copy-start | bytes 484
  7.2 114.7 %copy-start.3 = (bf16[384,1024]{1,0:T(8,128)(2,1)S(1)}, bf16[384,1024]{1,0:T(8,128)(2,1)}, u32[]{:S(2)}) copy-start(bf16[384,1024]{1,0:T(8,128)(2,1)} %param.10) | copy-start | bytes 2359300
  7.2 114.6 %all-gather.2.cloned.1.call-start = ((), (), s32[]{:S(2)}) async-start(), calls=%async_computation.1 | async-start | bytes 17825792 | tf_op jit(solution)/shard_map/all_gather | solution.py:44
  7.9 357.6 %reduce-scatter.2.cloned.1.call-start = ((), (), s32[]{:S(2)}) async-start(), calls=%async_computation.2 | async-start | bytes 17825792 | tf_op jit(solution)/shard_map/reduce_scatter | solution.py:54
  154.3 9.1 %copy-start.4 = (f32[5120]{0:T(1024)S(1)}, f32[5120]{0:T(1024)}, u32[]{:S(2)}) copy-start(f32[5120]{0:T(1024)} %param.7) | copy-start | bytes 61444
  163.3 8.8 %copy-start = (f32[384,40,128]{0,2,1:T(8,128)S(1)}, f32[384,40,128]{0,2,1:T(8,128)}, u32[]{:S(2)}) copy-start(f32[384,40,128]{0,2,1:T(8,128)} %copy.16) | copy-start | bytes 23592964
  163.3 8.8 %copy-start.1 = (bf16[384,5120]{0,1:T(8,128)(2,1)S(1)}, bf16[384,5120]{0,1:T(8,128)(2,1)}, u32[]{:S(2)}) copy-start(bf16[384,5120]{0,1:T(8,128)(2,1)} %copy.12) | copy-start | bytes 11796484
  205.8 2.6 copy-start.2
  220.0 73.0 %copy-start.5 = (f32[1024]{0:T(1024)S(1)}, f32[1024]{0:T(1024)}, u32[]{:S(2)}) copy-start(f32[1024]{0:T(1024)} %param.8) | copy-start | bytes 12292
Sparse Core Ops, SparseCore 0:
  10.5 111.3 all-gather.1
  220.1 145.3 reduce-scatter.1
where the time goes:
time: 446 us; the launch traced here: 444 us
  waiting for transfers between devices  164 us (37%)
  blocking collectives  139 us (31%)
  local copies, waits for them, and re-layouts  65.7 us (15%)
  matrix products  37.6 us (8%)
  other arithmetic  24.6 us (6%)
  between operations  14.2 us (3%)
    all_gather x1, waiting for transfers between devices, local(): whole_weight = lax.all_gather(key_weight, 'shard', axis=0, tiled=True)  104 us
    psum x1, blocking collectives, local(): lax.psum((group_sum, gain_group, bias_group), 'rep')  71.9 us
    psum x1, blocking collectives, local(): gain_group, bias_group = lax.psum((gain_part, bias_part), 'shard')  66.6 us
    reduce_scatter x1, waiting for transfers between devices, local(): lax.psum_scatter((lax.dot_general(normed_slots, cotangent, (((0,), (0,)),...  59.4 us
    gather x2, local copies, waits for them, and re-layouts, local(): jnp.take(grad_slots.reshape(row_count, slot_total, BLK), block_slot, axis=1)  17.8 us
    unnamed x16, local copies, waits for them, and re-layouts  15.2 us
    gather x2, local copies, waits for them, and re-layouts, local(): jnp.take(normed_blocks, jnp.maximum(block_of_slot, 0), axis=1)  14.7 us
    dot_general x1, matrix products, local(): jnp.dot(normed_slots, whole_weight, preferred_element_type=jnp.float32)  13.1 us
  transfers between devices with their start and end apart: 2, of which 2 were waited for; matrix products, arithmetic and copies ran while one was open for 7% of the time, Pallas kernels for 0%

commit v1 on v0

v1 whole, which is shorter than its diff:
```python
import functools

import jax
import jax.numpy as jnp
from jax import lax
from jax.experimental import pallas as pl
from jax.experimental.pallas import tpu as pltpu
from jax.sharding import PartitionSpec as P

MESH = pl.DeviceIdType.MESH
BLK = 128
EPS = 1e-06
HALF = 20
PARTS = (
    (0, 7, 4, (0, 1, 2)),
    (7, 7, 3, (1, 2, 0)),
    (14, 6, 3, (2, 0, 1)),
)
BF = jnp.bfloat16
F32 = jnp.float32


class Place:
    def __init__(self):
        big = lax.axis_index("shard")
        rep = lax.axis_index("rep")
        self.big, self.rep = big, rep
        self.c = lax.rem(big, 2)
        self.s = lax.div(big, 2)
        self.z = lax.rem(self.s, 4)
        xh = lax.div(big, 8)
        xl = lax.div(rep, 4)
        self.xl = xl
        self.x = xh * 2 + xl
        self.y = lax.rem(rep, 4)
        self.pos = (self.x, self.y, self.z)

    def at(self, axis, step):
        return lax.rem(self.pos[axis] + step, 4)

    def device(self, pos, c):
        x, y, z = pos
        big = (lax.div(x, 2) * 4 + z) * 2 + c
        return (big, lax.rem(x, 2) * 4 + y)

    def ring(self, axis, step):
        pos = list(self.pos)
        pos[axis] = self.at(axis, step)
        return self.device(pos, self.c)

    def partner(self):
        return (self.s * 2 + 1 - self.c, self.rep)

    def x_pair(self):
        return (self.big, (1 - self.xl) * 4 + self.y)

    def group(self):
        for k in range(8):
            for d in range(2):
                if k == 0 and d == 0:
                    continue
                core = self.c if d == 0 else 1 - self.c
                yield k, d, (lax.rem(self.s + k, 8) * 2 + core, self.rep)


class Wires:
    def __init__(self, send, recv, limit):
        self.send, self.recv, self.limit, self.n, self.open = send, recv, limit, 0, []

    def put(self, src, dst, device):
        i = self.n
        self.n += 1
        assert i < self.limit, "sems"
        copy = pltpu.make_async_remote_copy(
            src_ref=src, dst_ref=dst, send_sem=self.send.at[i], recv_sem=self.recv.at[i],
            device_id=device, device_id_type=MESH,
        )
        copy.start()
        self.open.append(copy)
        return copy

    def drain(self):
        for copy in self.open:
            copy.wait_send()
        self.open = []


def greet(place):
    barrier = pltpu.get_barrier_semaphore()
    peers = [device for _, _, device in place.group()]
    for axis in (0, 1):
        peers += [place.ring(axis, 1), place.ring(axis, 3)]
    peers.append(place.ring(1, 2))
    for device in peers:
        pl.semaphore_signal(barrier, inc=1, device_id=device, device_id_type=MESH)
    pl.semaphore_wait(barrier, len(peers))


def locate(place, order, k, v, done, later):
    out = [None] * 3
    for j, axis in enumerate(order):
        out[axis] = v if j == k else (done(axis) if j < k else later(axis))
    return tuple(out)


class Gather:
    def __init__(self, place, wires, w):
        self.place, self.wires, self.w = place, wires, w
        self.base = place.c * HALF
        self.stage = {}
        self.pair = []

    def view(self, p, k, v, first, count):
        off, nb, h, order = PARTS[p]
        pos = self.place.pos
        idx = locate(self.place, order, k, v, lambda a: slice(None), lambda a: pos[a])
        return self.w.at[idx + (pl.ds(self.base + off + first, count),)]

    def move(self, p, k, v, first, count, device):
        ref = self.view(p, k, v, first, count)
        return self.wires.put(ref, ref, device)

    def start(self, p, k):
        off, nb, h, order = PARTS[p]
        place, axis = self.place, order[k]
        me = place.pos[axis]
        up, down = place.ring(axis, 1), place.ring(axis, 3)
        u0 = self.move(p, k, me, 0, h, up)
        d1 = self.move(p, k, me, h, nb - h, down)
        u1 = self.move(p, k, me, h, nb - h, up)
        d0 = self.move(p, k, me, 0, h, down)
        self.stage[p, k] = [u0, d1, u1, d0]

    def share(self, p, k, v, first, count):
        if k == 2:
            self.pair.append(self.move(p, k, v, first, count, self.place.partner()))

    def forward(self, p, k):
        off, nb, h, order = PARTS[p]
        place, axis = self.place, order[k]
        u0, d1, u1, d0 = self.stage[p, k]
        below, above = place.at(axis, 3), place.at(axis, 1)
        u0.wait_recv()
        f0 = self.move(p, k, below, 0, h, place.ring(axis, 1))
        self.share(p, k, below, 0, h)
        d1.wait_recv()
        f1 = self.move(p, k, above, h, nb - h, place.ring(axis, 3))
        self.share(p, k, above, h, nb - h)
        self.stage[p, k] += [f0, f1]

    def finish(self, p, k):
        off, nb, h, order = PARTS[p]
        place, axis = self.place, order[k]
        u0, d1, u1, d0, f0, f1 = self.stage[p, k]
        below, above, across = place.at(axis, 3), place.at(axis, 1), place.at(axis, 2)
        u1.wait_recv()
        self.share(p, k, below, h, nb - h)
        d0.wait_recv()
        self.share(p, k, above, 0, h)
        f0.wait_recv()
        self.share(p, k, across, 0, h)
        f1.wait_recv()
        self.share(p, k, across, h, nb - h)
        if k == 1:
            self.share(p, 2, place.pos[order[2]], 0, nb)


def rest_of(t, count):
    if count == 2:
        return (lax.div(t, 4), lax.rem(t, 4))
    return (t,) if count == 1 else ()


class Scatter:
    def __init__(self, place, wires, g, bufs):
        self.place, self.wires, self.g, self.bufs = place, wires, g, bufs
        self.base = place.c * HALF
        self.stage = {}

    def index(self, p, k, v, later):
        order = PARTS[p][3]
        pos = self.place.pos
        return locate(self.place, order, k, v, lambda a: pos[a], later)

    def view(self, p, k, v, first, count):
        idx = self.index(p, k, v, lambda a: slice(None))
        return self.g.at[idx + (pl.ds(self.base + PARTS[p][0] + first, count),)]

    def tile(self, p, k, v, rest, first, count):
        order = PARTS[p][3]
        later = sorted(order[k + 1:])
        idx = self.index(p, k, v, lambda a: rest[later.index(a)])
        return idx + (pl.ds(self.base + PARTS[p][0] + first, count),)

    def buf(self, p, k, which):
        return self.bufs[p][k][which]

    def start(self, p, k):
        off, nb, h, order = PARTS[p]
        place, axis = self.place, order[k]
        put, full = self.wires.put, (slice(None),) * (2 - k)
        up, down = place.ring(axis, 1), place.ring(axis, 3)
        over, under = place.at(axis, 1), place.at(axis, 3)
        across = place.at(axis, 2)
        ta, tb, fm, fp = self.bufs[p][k]
        a = put(self.view(p, k, across, 0, h), ta, up)
        b = put(self.view(p, k, across, h, nb - h), tb, down)
        u = put(self.view(p, k, over, h, nb - h), fm.at[full + (pl.ds(h, nb - h),)], up)
        d = put(self.view(p, k, under, 0, h), fp.at[full + (pl.ds(0, h),)], down)
        self.stage[p, k] = [a, b, u, d]

    def forward(self, p, k):
        off, nb, h, order = PARTS[p]
        place, axis = self.place, order[k]
        put, full = self.wires.put, (slice(None),) * (2 - k)
        up, down = place.ring(axis, 1), place.ring(axis, 3)
        over, under = place.at(axis, 1), place.at(axis, 3)
        ta, tb, fm, fp = self.bufs[p][k]
        a, b, u, d = self.stage[p, k]
        g = self.g

        def add(t, v, buf, first, count):
            rest = rest_of(t, 2 - k)
            idx = self.tile(p, k, v, rest, first, count)
            g[idx] = g[idx] + buf[rest]

        a.wait_recv()
        pl.loop(0, 4 ** (2 - k))(lambda t: add(t, over, ta, 0, h))
        fa = put(self.view(p, k, over, 0, h), fm.at[full + (pl.ds(0, h),)], up)
        b.wait_recv()
        pl.loop(0, 4 ** (2 - k))(lambda t: add(t, under, tb, h, nb - h))
        fb = put(self.view(p, k, under, h, nb - h), fp.at[full + (pl.ds(h, nb - h),)], down)
        self.stage[p, k] += [fa, fb]

    def finish(self, p, k):
        off, nb, h, order = PARTS[p]
        me = self.place.pos[order[k]]
        ta, tb, fm, fp = self.bufs[p][k]
        a, b, u, d, fa, fb = self.stage[p, k]
        g = self.g
        for copy in (u, d, fa, fb):
            copy.wait_recv()

        def add(t):
            rest = rest_of(t, 2 - k)
            idx = self.tile(p, k, me, rest, 0, nb)
            total = g[idx].astype(F32) + fm[rest].astype(F32) + fp[rest].astype(F32)
            g[idx] = total.astype(BF)

        pl.loop(0, 4 ** (2 - k))(add)


def scatter_scratch():
    out = []
    for p in range(3):
        _, nb, h, _ = PARTS[p]
        for k in range(3):
            lead = (4,) * (2 - k)
            out += [pltpu.VMEM(lead + (n, 16, 128), BF) for n in (h, nb - h, nb, nb)]
    return out


def scatter_bufs(flat):
    return [[flat[(p * 3 + k) * 4:(p * 3 + k) * 4 + 4] for k in range(3)] for p in range(3)]


class Small:
    def __init__(self, place, wires, first, rest):
        self.place, self.wires, self.first, self.rest = place, wires, first, rest
        self.sent = []

    def start(self, k, value):
        place = self.place
        if k == 0:
            self.first[place.c] = value
            own = self.first.at[place.c]
            self.sent = [self.wires.put(own, own, place.partner())]
            return
        axis = k - 1
        self.rest[axis, place.pos[axis]] = value
        own = self.rest.at[axis, place.pos[axis]]
        self.sent = [self.wires.put(own, own, place.ring(axis, step)) for step in (1, 3, 2)]

    def finish(self, k):
        for copy in self.sent:
            copy.wait_recv()
        if k == 0:
            return self.first[0] + self.first[1]
        t = self.rest
        return (t[k - 1, 0] + t[k - 1, 1]) + (t[k - 1, 2] + t[k - 1, 3])


def gather_kernel(slots_ref, kw_ref, out_ref, w, kws, held, send, recv, local):
    place = Place()
    wires = Wires(send, recv, 100)
    loads = []
    for t in range(8):
        load = pltpu.make_async_copy(kw_ref.at[:, place.rep, :, pl.ds(t * 128, 128)], kws.at[t], local.at[t])
        load.start()
        loads.append(load)
    greet(place)
    for load in loads:
        load.wait()
    mine = held.at[pl.ds(place.big * 4, 4)]
    come = [wires.put(kws.at[lax.rem(place.s + k, 8)], mine, device) for k, _, device in place.group()]
    held[pl.ds(place.big * 4, 4)] = kws[place.s]
    for copy in come:
        copy.wait_recv()

    @pl.loop(0, HALF)
    def _(t):
        b = place.c * HALF + t
        w[place.x, place.y, place.z, b] = held[slots_ref[b]]

    gather = Gather(place, wires, w)
    for p in range(3):
        gather.start(p, 0)
    for k in range(3):
        for p in range(3):
            gather.forward(p, k)
        for p in range(3):
            gather.finish(p, k)
            if k < 2:
                gather.start(p, k + 1)
    for copy in gather.pair:
        copy.wait_recv()
    stores = []
    for i in range(64):
        x, y, z = i // 16, i // 4 % 4, i % 4
        store = pltpu.make_async_copy(
            w.at[x, y, z],
            out_ref.at[:, (x % 2) * 4 + y, :, pl.ds((x // 2 * 4 + z) * 128, 128)],
            local.at[i],
        )
        store.start()
        stores.append(store)
    for store in stores:
        store.wait()
    wires.drain()


def scatter_kernel(owner_ref, part_ref, small_ref, out_ref, total_ref, g, half, slot, seen, fin,
                   first, rest, send, recv, local, *flat):
    place = Place()
    wires = Wires(send, recv, 130)
    loads = []
    for i in range(64):
        x, y, z = i // 16, i // 4 % 4, i % 4
        load = pltpu.make_async_copy(
            part_ref.at[:, (x % 2) * 4 + y, :, pl.ds((x // 2 * 4 + z) * 128, 128)],
            g.at[x, y, z],
            local.at[i],
        )
        load.start()
        loads.append(load)
    greet(place)
    for load in loads:
        load.wait()
    small = Small(place, wires, first, rest)
    small.start(0, small_ref[...])
    other = (1 - place.c) * HALF
    full = (slice(None),) * 3
    swap = []
    for off, nb, _, _ in PARTS:
        swap.append(wires.put(
            g.at[full + (pl.ds(other + off, nb),)], half.at[full + (pl.ds(off, nb),)], place.partner()))
    scatter = Scatter(place, wires, g, scatter_bufs(flat))
    mine = place.c * HALF
    for p, (off, nb, _, _) in enumerate(PARTS):
        swap[p].wait_recv()

        @pl.loop(0, 64)
        def _(t):
            i = (lax.div(t, 16), lax.rem(lax.div(t, 4), 4), lax.rem(t, 4))
            own = i + (pl.ds(mine + off, nb),)
            g[own] = g[own] + half[i + (pl.ds(off, nb),)]

        scatter.start(p, 0)
    for k in range(3):
        small.start(k + 1, small.finish(k))
        for p in range(3):
            scatter.forward(p, k)
        for p in range(3):
            scatter.finish(p, k)
            if k < 2:
                scatter.start(p, k + 1)
    total_ref[...] = small.finish(3)

    @pl.loop(0, 64)
    def _(t):
        b = owner_ref[t]
        ours = jnp.logical_and(b >= mine, b < mine + HALF)
        value = g[place.x, place.y, place.z, jnp.maximum(b, 0)]
        slot[t] = jnp.where(ours, value, jnp.zeros_like(value))

    come = []
    for _, _, device in place.group():
        come.append(wires.put(slot.at[pl.ds(device[0] * 4, 4)], seen.at[place.c, place.s], device))
    seen[place.c, place.s] = slot[pl.ds(place.big * 4, 4)]
    for copy in come:
        copy.wait_recv()
    for t in range(8):
        fin[place.xl, place.y, :, t] = seen[0, t] + seen[1, t]
    lo, hi = pl.ds(0, 2), pl.ds(2, 2)
    yup, ydown = place.ring(1, 1), place.ring(1, 3)
    below, above = place.at(1, 3), place.at(1, 1)

    def move(x, y, part, device):
        ref = fin.at[x, y, part]
        return wires.put(ref, ref, device)

    xl, y = place.xl, place.y
    every = slice(None)
    px = move(xl, y, lo, place.x_pair())
    hu = move(xl, y, hi, yup)
    hd = move(xl, y, hi, ydown)
    px.wait_recv()
    lu = [move(every, y, pl.ds(i, 1), yup) for i in (0, 1)]
    ld = [move(every, y, pl.ds(i, 1), ydown) for i in (1, 0)]
    hu.wait_recv()
    hfu = move(xl, below, pl.ds(2, 1), yup)
    hd.wait_recv()
    hfd = move(xl, above, pl.ds(3, 1), ydown)
    hfu.wait_recv()
    hfd.wait_recv()
    qx = move(xl, every, hi, place.x_pair())
    lu[0].wait_recv()
    lfu = move(every, below, pl.ds(0, 1), yup)
    ld[0].wait_recv()
    lfd = move(every, above, pl.ds(1, 1), ydown)
    for copy in (lu[1], ld[1], lfu, lfd, qx):
        copy.wait_recv()

    @pl.loop(0, 32)
    def _(t):
        i, r = lax.div(t, 8), lax.rem(t, 8)
        for j in range(8):
            out_ref[i, r, :, j * 128:(j + 1) * 128] = fin[lax.div(r, 4), lax.rem(r, 4), i, j].astype(F32)

    wires.drain()


VM = pl.BlockSpec(memory_space=pltpu.VMEM)
SM = pl.BlockSpec(memory_space=pltpu.SMEM)
ANY = pl.BlockSpec(memory_space=pl.ANY)
LIMIT = 64 * 1024 * 1024 - 65536


def gather_weights(block_slot, key_weight):
    return pl.pallas_call(
        gather_kernel,
        out_shape=jax.ShapeDtypeStruct((40, 8, 16, 1024), BF),
        in_specs=[SM, ANY],
        out_specs=ANY,
        scratch_shapes=[
            pltpu.VMEM((4, 4, 4, 40, 16, 128), BF),
            pltpu.VMEM((8, 4, 16, 128), BF),
            pltpu.VMEM((64, 16, 128), BF),
            pltpu.SemaphoreType.DMA((100,)),
            pltpu.SemaphoreType.DMA((100,)),
            pltpu.SemaphoreType.DMA((64,)),
        ],
        compiler_params=pltpu.CompilerParams(collective_id=0, has_side_effects=True, vmem_limit_bytes=LIMIT),
        name="gather",
    )(block_slot, key_weight.reshape(4, 8, 16, 1024))


def scatter_grads(owner, part, small):
    return pl.pallas_call(
        scatter_kernel,
        out_shape=(
            jax.ShapeDtypeStruct((4, 8, 16, 1024), F32),
            jax.ShapeDtypeStruct((48, 128), F32),
        ),
        in_specs=[SM, ANY, VM],
        out_specs=(VM, VM),
        scratch_shapes=[
            pltpu.VMEM((4, 4, 4, 40, 16, 128), BF),
            pltpu.VMEM((4, 4, 4, 20, 16, 128), BF),
            pltpu.VMEM((64, 16, 128), BF),
            pltpu.VMEM((2, 8, 4, 16, 128), BF),
            pltpu.VMEM((2, 4, 4, 8, 16, 128), BF),
            pltpu.VMEM((2, 48, 128), F32),
            pltpu.VMEM((3, 4, 48, 128), F32),
            pltpu.SemaphoreType.DMA((130,)),
            pltpu.SemaphoreType.DMA((130,)),
            pltpu.SemaphoreType.DMA((64,)),
        ] + scatter_scratch(),
        compiler_params=pltpu.CompilerParams(collective_id=1, has_side_effects=True, vmem_limit_bytes=LIMIT),
        name="scatter",
    )(owner, part.reshape(40, 8, 16, 1024), small)


def local(tokens, norm_gain, key_bias, key_weight, cotangent, block_slot):
    row_count, width = tokens.shape
    grad_scale = float(row_count * lax.axis_size("shard") * lax.axis_size("rep")) ** (-0.5)
    slots = jnp.arange(64, dtype=jnp.int32)
    hit = block_slot[None, :] == slots[:, None]
    owner = jnp.max(jnp.where(hit, jnp.arange(40, dtype=jnp.int32)[None, :], -1), axis=1)
    weight = gather_weights(block_slot, key_weight).reshape(width, 1024)
    values = tokens.astype(F32)
    inv_rms = lax.rsqrt(jnp.mean(values * values, axis=-1, keepdims=True) + EPS)
    normed = (values * inv_rms * norm_gain).astype(BF)
    forward = jnp.dot(normed, weight, preferred_element_type=F32)
    projected = (forward + key_bias).astype(BF)
    grad_normed = lax.dot_general(cotangent, weight, (((1,), (1,)), ((), ())), preferred_element_type=F32)
    scaled = grad_normed * norm_gain
    inner = jnp.mean(scaled * values, axis=-1, keepdims=True)
    token_grad = (inv_rms * (scaled - values * inv_rms * inv_rms * inner)).astype(BF)
    part = (
        lax.dot_general(normed, cotangent, (((0,), (0,)), ((), ())), preferred_element_type=F32) * grad_scale
    ).astype(BF)
    gain_part = jnp.sum(grad_normed * values * inv_rms, axis=0) * grad_scale
    bias_part = jnp.sum(cotangent.astype(F32), axis=0) * grad_scale
    small = jnp.concatenate([gain_part, bias_part]).reshape(48, 128)
    sums, total = scatter_grads(owner, part, small)
    total = total.reshape(-1)
    return (projected, token_grad, sums.reshape(512, 1024), total[:width], total[width:])


def solution(mesh):
    return jax.shard_map(
        local,
        mesh=mesh,
        in_specs=(
            P(("shard", "rep"), None),
            P(),
            P(),
            P("shard", None),
            P(("shard", "rep"), None),
            P(),
        ),
        out_specs=(
            P(("shard", "rep"), None),
            P(("shard", "rep"), None),
            P("shard", None),
            P(),
            P(),
        ),
        check_vma=False,
    )
```

time: 446 us -> 181 us (0.41)
  waiting for transfers between devices: 164 us -> 0 us
  blocking collectives: 139 us -> 0 us
  Pallas kernels: 0 us -> 125 us
  local copies, waits for them, and re-layouts: 65.7 us -> 18.4 us
  other arithmetic: 24.6 us -> 8.49 us
  between operations: 14.2 us -> 0.75 us
  matrix products: 37.6 us -> 27.7 us
    psum x2 -> x0, blocking collectives: 139 us -> none  [the longest x1 71.9 us: local(): lax.psum((group_sum, gain_group, bias_group), 'rep')]
    pallas_call x0 -> x2, Pallas kernels: none -> 125 us  [the longest x1 73.2 us: scatter_grads(): pl.pallas_call(scatter_kernel, out_shape=(jax.ShapeDtypeStruct((4, 8, 16,...]
    all_gather x1 -> x0, waiting for transfers between devices: 104 us -> none  [local(): whole_weight = lax.all_gather(key_weight, 'shard', axis=0, tiled=True)]
    reduce_scatter x1 -> x0, waiting for transfers between devices: 59.4 us -> none  [local(): lax.psum_scatter((lax.dot_general(normed_slots, cotangent, (((0,), (0,)),...]
    gather x4 -> x0, local copies, waits for them, and re-layouts: 32.6 us -> none  [the longest x2 17.8 us: local(): jnp.take(grad_slots.reshape(row_count, slot_total, BLK), block_slot, axis=1)]
    reshape x2 -> x0, local copies, waits for them, and re-layouts: 17.1 us -> none  [the longest x1 10.8 us: local(): grad_slots.reshape(row_count, slot_total, BLK)]
    dot_general x3, matrix products: 37.6 us -> 27.7 us  [the longest x1 10.5 us: local(): forward = jnp.dot(normed, weight, preferred_element_type=F32)]
    reduce_sum x3 -> x2, other arithmetic: 12 us -> 3.32 us  [the longest x1 3.18 us: local(): inv_rms = lax.rsqrt(jnp.mean(values * values, axis=-1, keepdims=True) + EPS)]
  transfers between devices with their start and end apart: 2 -> 0, of which waited for: 2 -> 0; matrix products, arithmetic and copies ran while one was open for 7% -> 0% of each run, Pallas kernels for 0% -> 0%
where the time goes in v1:
time: 181 us
  Pallas kernels  125 us (69%)
  matrix products  27.7 us (15%)
  local copies, waits for them, and re-layouts  18.4 us (10%)
  other arithmetic  8.49 us (5%)
    pallas_call x1, Pallas kernels, scatter_grads(): pl.pallas_call(scatter_kernel, out_shape=(jax.ShapeDtypeStruct((4, 8, 16,...  73.2 us
    pallas_call x1, Pallas kernels, gather_weights(): pl.pallas_call(gather_kernel, out_shape=jax.ShapeDtypeStruct((40, 8, 16,...  52.2 us
    unnamed x19, local copies, waits for them, and re-layouts  15.8 us
    dot_general x1, matrix products, local(): forward = jnp.dot(normed, weight, preferred_element_type=F32)  10.5 us
    dot_general x1, matrix products, local(): lax.dot_general(normed, cotangent, (((0,), (0,)), ((), ())), preferred_el...  10.5 us
    dot_general x1, matrix products, local(): lax.dot_general(cotangent, weight, (((1,), (1,)), ((), ())), preferred_el...  6.68 us
    convert_element_type x1, other arithmetic, local(): (inv_rms * (scaled - values * inv_rms * inv_rms * inner)).astype(BF)  3.94 us

profile of v1, /device:TPU:0, one launch (start us, length us, event | category | flops | bytes accessed | tf_op | source)
XLA Modules:
  0.0 180.7 jit_solution(5688989493104930783)
XLA Ops:
  0.6 52.2 %gather.1 = bf16[40,8,16,1024]{3,2,1,0:T(8,128)(2,1)} custom-call(s32[40]{0:T(128)} %slots_ref.1, bf16[4,8,16,1024]{3,2,1,0:T(8,128)(2,1)} %bitcast.27), custom_call_target="tpu_custom_call" | custom-call | tf_op jit(solution)/shard_map/gather/pallas_call | solution.py:450
  52.9 0.0 copy-start.2
  52.9 0.0 copy-start.4
  52.9 6.3 %copy.13 = bf16[384,5120]{0,1:T(8,128)(2,1)} copy(bf16[384,5120]{1,0:T(8,128)(2,1)} %param.6) | data formatting | bytes 7864320 | tf_op args[0]
  59.2 0.0 slice-start
  59.2 3.2 %fusion.7 = f32[384]{0:T(512)S(1)} fusion(bf16[384,5120]{0,1:T(8,128)(2,1)} %copy.13), kind=kLoop, calls=%fused_computation.12 | loop fusion | flops 5897856 | bytes 3933696 | tf_op jit(solution)/shard_map/reduce_sum | solution.py:502
  62.4 0.0 copy-done.2
  62.4 0.0 copy-done.4
  62.4 0.0 copy-start
  62.4 0.0 slice-start.1
  62.4 0.0 slice-start.2
  62.4 0.0 copy-start.1
  62.4 10.5 %add_convert_fusion = bf16[384,1024]{1,0:T(8,128)(2,1)} fusion(bf16[5120,1024]{1,0:T(8,128)(2,1)} %bitcast.22, bf16[384,5120]{0,1:T(8,128)(2,1)} %copy.13, f32[5120]{0:T(1024)S(1)} %copy-done.2, f32[384]{0:T(512)S(1)} %add_rsqrt_fusion, f32[1024]{0:T(1024)S(1)} %copy-done.4), kind=kOutput, calls=%fused_computation.18 | convolution fusion | flops 4035182592 | bytes 15230464 | tf_op jit(solution)/shard_map/dot_general | solution.py:504
  72.9 0.0 slice-done
  72.9 0.0 copy-done
  73.0 0.0 slice-done.1
  73.0 0.0 slice-done.2
  73.0 0.0 copy-done.1
  73.0 6.7 %fusion.10 = (f32[5120]{0:T(1024)S(1)}, f32[384]{0:T(512)S(1)}, f32[5120,384]{1,0:T(8,128)S(1)}) fusion(bf16[384,5120]{0,1:T(8,128)(2,1)S(1)} %copy-done, f32[384]{0:T(512)S(1)} %add_rsqrt_fusion, f32[5120]{0:T(1024)S(1)} %copy-done.2, bf16[5120,1024]{1,0:T(8,128)(2,1)S(1)} %bitcast.25, bf16[384,1024]{1,0:T(8,128)(2,1)S(1)} %copy-done.1), kind=kOutput, calls=%fused_computation.15 | convolution fusion | flops 4040288768 | bytes 23112704 | tf_op jit(solution)/shard_map/dot_general | solution.py:506
  79.7 3.9 %fusion.6 = bf16[384,5120]{0,1:T(8,128)(2,1)} fusion(bf16[384,5120]{0,1:T(8,128)(2,1)S(1)} %copy-done, f32[5120,384]{1,0:T(8,128)S(1)} %get-tuple-element.21, f32[384]{0:T(512)S(1)} %broadcast_multiply_fusion.2, f32[5120]{0:T(1024)S(1)} %copy-done.2, f32[384]{0:T(512)S(1)} %add_rsqrt_fusion), kind=kLoop, calls=%fused_computation.11 | loop fusion | flops 15728640 | bytes 15752192 | tf_op jit(solution)/shard_map/convert_element_type | solution.py:509
  83.6 0.0 copy-start.3
  83.6 6.3 %copy.14 = bf16[384,5120]{1,0:T(8,128)(2,1)} copy(bf16[384,5120]{0,1:T(8,128)(2,1)} %fusion.6) | data formatting | bytes 7864320
  89.9 0.0 copy-done.3
  89.9 0.6 select_reduce_fusion.owner_ref
  90.5 10.5 %multiply_convert_fusion = bf16[5120,1024]{1,0:T(8,128)(2,1)} fusion(bf16[384,1024]{1,0:T(8,128)(2,1)S(1)} %copy-done.1, bf16[384,5120]{0,1:T(8,128)(2,1)} %copy.13, f32[5120]{0:T(1024)S(1)} %copy-done.2, f32[384]{0:T(512)S(1)} %add_rsqrt_fusion), kind=kOutput, calls=%fused_computation | convolution fusion | flops 4044881920 | bytes 15226368 | tf_op jit(solution)/shard_map/dot_general | solution.py:511
  101.0 0.1 convert_reduce_fusion
  101.2 0.6 maximum_bitcast_fusion.small_ref
  101.8 73.2 %scatter.1 = (f32[4,8,16,1024]{3,2,1,0:T(8,128)}, f32[48,128]{1,0:T(8,128)}) custom-call(s32[64]{0:T(128)} %select_reduce_fusion.owner_ref, bf16[40,8,16,1024]{3,2,1,0:T(8,128)(2,1)} %bitcast.21, f32[48,128]{1,0:T(8,128)} %maximum_bitcast_fusion.small_ref), custom_call_target="tpu_custom_call" | custom-call | tf_op jit(solution)/shard_map/scatter/pallas_call | solution.py:469
  174.9 1.3 slice_bitcast_fusion
  176.3 1.3 slice_bitcast_fusion.1
  177.6 3.2 %copy.16 = f32[512,1024]{1,0:T(8,128)} copy(f32[512,1024]{1,0:T(8,128)} %bitcast.26) | data formatting | bytes 4194304
  (5 shorter events, 0.0 us)
Async XLA Ops:
  52.9 9.5 %copy-start.2 = (f32[5120]{0:T(1024)S(1)}, f32[5120]{0:T(1024)}, u32[]{:S(2)}) copy-start(f32[5120]{0:T(1024)} %param.7) | copy-start | bytes 61444
  52.9 9.5 %copy-start.4 = (f32[1024]{0:T(1024)S(1)}, f32[1024]{0:T(1024)}, u32[]{:S(2)}) copy-start(f32[1024]{0:T(1024)} %param.8) | copy-start | bytes 12292
  59.2 13.8 %slice-start = ((s8[10485760]{0:T(1024)(128)(4,1)}), s8[4194304]{0:T(1024)(128)(4,1)S(1)}, s32[]{:S(2)}) async-start(s8[10485760]{0:T(1024)(128)(4,1)} %bitcast.23), calls=%async_computation | async-start | bytes 8388608
  62.4 10.6 %copy-start = (bf16[384,5120]{0,1:T(8,128)(2,1)S(1)}, bf16[384,5120]{0,1:T(8,128)(2,1)}, u32[]{:S(2)}) copy-start(bf16[384,5120]{0,1:T(8,128)(2,1)} %copy.13) | copy-start | bytes 11796484
  62.4 10.6 %slice-start.1 = ((s8[10485760]{0:T(1024)(128)(4,1)}), s8[4194304]{0:T(1024)(128)(4,1)S(1)}, s32[]{:S(2)}) async-start(s8[10485760]{0:T(1024)(128)(4,1)} %bitcast.23), calls=%async_computation.1 | async-start | bytes 8388608
  62.4 10.6 %slice-start.2 = ((s8[10485760]{0:T(1024)(128)(4,1)}), s8[2097152]{0:T(1024)(128)(4,1)S(1)}, s32[]{:S(2)}) async-start(s8[10485760]{0:T(1024)(128)(4,1)} %bitcast.23), calls=%async_computation.2 | async-start | bytes 4194304
  62.4 10.6 %copy-start.1 = (bf16[384,1024]{1,0:T(8,128)(2,1)S(1)}, bf16[384,1024]{1,0:T(8,128)(2,1)}, u32[]{:S(2)}) copy-start(bf16[384,1024]{1,0:T(8,128)(2,1)} %param.10) | copy-start | bytes 2359300
  83.6 6.3 %copy-start.3 = (s32[40]{0:T(128)S(1)}, s32[40]{0:T(128)}, u32[]{:S(2)}) copy-start(s32[40]{0:T(128)} %slots_ref.1) | copy-start | bytes 484

commit v2 on v1

--- a/solution.py
+++ b/solution.py
@@ -290,20 +290,56 @@
         return (t[k - 1, 0] + t[k - 1, 1]) + (t[k - 1, 2] + t[k - 1, 3])
 
 
-def gather_kernel(slots_ref, kw_ref, out_ref, w, kws, held, send, recv, local):
+WIDTH = 5120
+KEYS = 1024
+ROWS = 384
+
+
+def fused_kernel(slots_ref, owner_ref, tok_ref, gain_ref, bias_ref, kw_ref, cot_ref,
+                 proj_out, grad_out, slab_out, total_ref,
+                 w, kws, held, g, half, slot, seen, fin, first, rest,
+                 tok, normed, cot, proj, inv, coef, small_v, send, recv, local, *flat):
     place = Place()
-    wires = Wires(send, recv, 100)
+    wires = Wires(send, recv, 200)
+    grad_scale = float(ROWS * 128) ** (-0.5)
     loads = []
-    for t in range(8):
-        load = pltpu.make_async_copy(kw_ref.at[:, place.rep, :, pl.ds(t * 128, 128)], kws.at[t], local.at[t])
-        load.start()
-        loads.append(load)
+
+    def load(src, dst):
+        copy = pltpu.make_async_copy(src, dst, local.at[len(loads)])
+        copy.start()
+        loads.append(copy)
+        return copy
+
+    slabs = [load(kw_ref.at[:, place.rep, :, pl.ds(t * 128, 128)], kws.at[t]) for t in range(8)]
+    rows = [load(tok_ref.at[pl.ds(i * 64, 64)], tok.at[pl.ds(i * 64, 64)]) for i in range(6)]
+    cots = load(cot_ref, cot)
     greet(place)
-    for load in loads:
-        load.wait()
+    for copy in slabs:
+        copy.wait()
     mine = held.at[pl.ds(place.big * 4, 4)]
     come = [wires.put(kws.at[lax.rem(place.s + k, 8)], mine, device) for k, _, device in place.group()]
     held[pl.ds(place.big * 4, 4)] = kws[place.s]
+
+    def norm(i):
+        rows[i].wait()
+
+        @pl.loop(i * 4, i * 4 + 4)
+        def _(t):
+            r = pl.ds(pl.multiple_of(t * 16, 16), 16)
+            acc = [jnp.zeros((16, 128), F32)] * 4
+            for j in range(40):
+                v = tok[r, j * 128:(j + 1) * 128].astype(F32)
+                acc[j % 4] = acc[j % 4] + v * v
+            total = jnp.sum((acc[0] + acc[1]) + (acc[2] + acc[3]), axis=1, keepdims=True)
+            scale = jnp.broadcast_to(lax.rsqrt(total * (1.0 / WIDTH) + EPS), (16, 128))
+            inv[r, :] = scale
+            for j in range(40):
+                col = slice(j * 128, (j + 1) * 128)
+                normed[r, col] = (tok[r, col].astype(F32) * scale * gain_ref[:, col]).astype(BF)
+
+    gather = Gather(place, wires, w)
+    for i in range(2):
+        norm(i)
     for copy in come:
         copy.wait_recv()
 
@@ -312,84 +348,140 @@
         b = place.c * HALF + t
         w[place.x, place.y, place.z, b] = held[slots_ref[b]]
 
-    gather = Gather(place, wires, w)
     for p in range(3):
         gather.start(p, 0)
-    for k in range(3):
-        for p in range(3):
-            gather.forward(p, k)
-        for p in range(3):
-            gather.finish(p, k)
-            if k < 2:
-                gather.start(p, k + 1)
-    for copy in gather.pair:
-        copy.wait_recv()
-    stores = []
-    for i in range(64):
-        x, y, z = i // 16, i // 4 % 4, i % 4
-        store = pltpu.make_async_copy(
-            w.at[x, y, z],
-            out_ref.at[:, (x % 2) * 4 + y, :, pl.ds((x // 2 * 4 + z) * 128, 128)],
-            local.at[i],
-        )
-        store.start()
-        stores.append(store)
-    for store in stores:
-        store.wait()
-    wires.drain()
-
-
-def scatter_kernel(owner_ref, part_ref, small_ref, out_ref, total_ref, g, half, slot, seen, fin,
-                   first, rest, send, recv, local, *flat):
-    place = Place()
-    wires = Wires(send, recv, 130)
-    loads = []
-    for i in range(64):
-        x, y, z = i // 16, i // 4 % 4, i % 4
-        load = pltpu.make_async_copy(
-            part_ref.at[:, (x % 2) * 4 + y, :, pl.ds((x // 2 * 4 + z) * 128, 128)],
-            g.at[x, y, z],
-            local.at[i],
-        )
-        load.start()
-        loads.append(load)
-    greet(place)
-    for load in loads:
-        load.wait()
-    small = Small(place, wires, first, rest)
-    small.start(0, small_ref[...])
-    other = (1 - place.c) * HALF
+    for i in range(2, 6):
+        norm(i)
+    for p in range(3):
+        gather.forward(p, 0)
+    cots.wait()
+    for j in range(8):
+        small_v[40 + j:41 + j, :] = jnp.sum(
+            cot[:, j * 128:(j + 1) * 128].astype(F32), axis=0, keepdims=True) * grad_scale
+
+    def partial(side, low, high):
+        @pl.loop(low, high)
+        def _(t):
+            b = side * HALF + 2 * t
+            left = normed[:, pl.ds(pl.multiple_of(b * 128, 128), 256)]
+            value = lax.dot_general(left, cot[...], (((0,), (0,)), ((), ())), preferred_element_type=F32)
+            value = (value * grad_scale).astype(BF)
+            for i in range(2):
+                for r in range(8):
+                    for q in range(8):
+                        g[q // 4 * 2 + r // 4, r % 4, q % 4, b + i] = value[
+                            i * 128 + r * 16:i * 128 + r * 16 + 16, q * 128:(q + 1) * 128]
+
+    pairs = ((0, 4), (4, 7), (7, 10))
+    swap = []
     full = (slice(None),) * 3
-    swap = []
-    for off, nb, _, _ in PARTS:
+
+    def exchange(p):
+        off, nb = PARTS[p][:2]
+        other = (1 - place.c) * HALF
         swap.append(wires.put(
             g.at[full + (pl.ds(other + off, nb),)], half.at[full + (pl.ds(off, nb),)], place.partner()))
+
     scatter = Scatter(place, wires, g, scatter_bufs(flat))
-    mine = place.c * HALF
-    for p, (off, nb, _, _) in enumerate(PARTS):
+    own = place.c * HALF
+
+    def merge(p):
+        off, nb = PARTS[p][:2]
         swap[p].wait_recv()
 
         @pl.loop(0, 64)
         def _(t):
             i = (lax.div(t, 16), lax.rem(lax.div(t, 4), 4), lax.rem(t, 4))
-            own = i + (pl.ds(mine + off, nb),)
-            g[own] = g[own] + half[i + (pl.ds(off, nb),)]
-
+            at = i + (pl.ds(own + off, nb),)
+            g[at] = g[at] + half[i + (pl.ds(off, nb),)]
+
+    partial(1 - place.c, *pairs[0])
+    exchange(0)
+    for p in range(3):
+        gather.finish(p, 0)
+        gather.start(p, 1)
+    partial(1 - place.c, *pairs[1])
+    exchange(1)
+    for p in range(3):
+        gather.forward(p, 1)
+    partial(1 - place.c, *pairs[2])
+    exchange(2)
+    for p in range(3):
+        gather.finish(p, 1)
+        gather.start(p, 2)
+    for p in range(3):
+        partial(place.c, *pairs[p])
+        merge(p)
         scatter.start(p, 0)
+    for p in range(3):
+        gather.forward(p, 2)
+    for p in range(3):
+        gather.finish(p, 2)
+    for copy in gather.pair:
+        copy.wait_recv()
+
+    coef[...] = jnp.zeros_like(coef)
+
+    @pl.loop(0, 4)
+    def _(n):
+        q = 2 * n
+        x0, z0 = lax.div(q, 4) * 2, lax.rem(q, 4)
+        right = jnp.concatenate(
+            [jnp.concatenate([w[x0 + r // 4, r % 4, z0, b], w[x0 + r // 4, r % 4, z0 + 1, b]], axis=1)
+             for b in range(40) for r in range(8)], axis=0)
+        value = jnp.dot(normed[...], right, preferred_element_type=F32)
+        col = pl.ds(pl.multiple_of(n * 256, 256), 256)
+        proj[:, col] = (value + bias_ref[:, col]).astype(BF)
+        both = value * cot[:, col].astype(F32)
+        coef[...] += both[:, :128] + both[:, 128:]
+
+    def store(src, dst):
+        copy = load(src, dst)
+        return copy
+
+    stores = [store(proj, proj_out)]
+    coef[...] = jnp.broadcast_to(
+        jnp.sum(coef[...], axis=1, keepdims=True), (ROWS, 128)) * inv[...] * (1.0 / WIDTH)
+
+    def backward(low, high):
+        @pl.loop(low, high)
+        def _(t):
+            b = 2 * t
+            right = jnp.concatenate(
+                [jnp.concatenate([w[q // 4 * 2 + r // 4, r % 4, q % 4, b + i] for q in range(8)], axis=1)
+                 for i in range(2) for r in range(8)], axis=0)
+            grad = lax.dot_general(cot[...], right, (((1,), (1,)), ((), ())), preferred_element_type=F32)
+            for i in range(2):
+                col = pl.ds(pl.multiple_of((b + i) * 128, 128), 128)
+                gn = grad[:, i * 128:(i + 1) * 128]
+                scale = inv[...]
+                unit = tok[:, col].astype(F32) * scale
+                small_v[pl.ds(b + i, 1), :] = jnp.sum(gn * unit, axis=0, keepdims=True) * grad_scale
+                tok[:, col] = (gn * gain_ref[:, col] * scale - unit * coef[...]).astype(BF)
+
+        col = pl.ds(low * 256, (high - low) * 256)
+        stores.append(store(tok.at[:, col], grad_out.at[:, col]))
+
+    small = Small(place, wires, first, rest)
+    for p in range(3):
+        scatter.forward(p, 0)
+    for i in range(4):
+        backward(i * 5, i * 5 + 5)
+    small.start(0, small_v[...])
     for k in range(3):
-        small.start(k + 1, small.finish(k))
-        for p in range(3):
-            scatter.forward(p, k)
+        if k:
+            for p in range(3):
+                scatter.forward(p, k)
         for p in range(3):
             scatter.finish(p, k)
             if k < 2:
                 scatter.start(p, k + 1)
-    total_ref[...] = small.finish(3)
+        small.start(k + 1, small.finish(k))
 
     @pl.loop(0, 64)
     def _(t):
         b = owner_ref[t]
-        ours = jnp.logical_and(b >= mine, b < mine + HALF)
+        ours = jnp.logical_and(b >= own, b < own + HALF)
         value = g[place.x, place.y, place.z, jnp.maximum(b, 0)]
         slot[t] = jnp.where(ours, value, jnp.zeros_like(value))
 
@@ -397,6 +489,7 @@
     for _, _, device in place.group():
         come.append(wires.put(slot.at[pl.ds(device[0] * 4, 4)], seen.at[place.c, place.s], device))
     seen[place.c, place.s] = slot[pl.ds(place.big * 4, 4)]
+    total_ref[...] = small.finish(3)
     for copy in come:
         copy.wait_recv()
     for t in range(8):
@@ -435,8 +528,10 @@
     def _(t):
         i, r = lax.div(t, 8), lax.rem(t, 8)
         for j in range(8):
-            out_ref[i, r, :, j * 128:(j + 1) * 128] = fin[lax.div(r, 4), lax.rem(r, 4), i, j].astype(F32)
-
+            slab_out[i, r, :, j * 128:(j + 1) * 128] = fin[lax.div(r, 4), lax.rem(r, 4), i, j]
+
+    for copy in stores:
+        copy.wait()
     wires.drain()
 
 
@@ -446,35 +541,21 @@
 LIMIT = 64 * 1024 * 1024 - 65536
 
 
-def gather_weights(block_slot, key_weight):
+def fused(block_slot, owner, tokens, gain, bias, key_weight, cotangent):
     return pl.pallas_call(
-        gather_kernel,
-        out_shape=jax.ShapeDtypeStruct((40, 8, 16, 1024), BF),
-        in_specs=[SM, ANY],
-        out_specs=ANY,
+        fused_kernel,
+        out_shape=(
+            jax.ShapeDtypeStruct((ROWS, KEYS), BF),
+            jax.ShapeDtypeStruct((ROWS, WIDTH), BF),
+            jax.ShapeDtypeStruct((4, 8, 16, 1024), BF),
+            jax.ShapeDtypeStruct((48, 128), F32),
+        ),
+        in_specs=[SM, SM, ANY, VM, VM, ANY, ANY],
+        out_specs=(ANY, ANY, VM, VM),
         scratch_shapes=[
             pltpu.VMEM((4, 4, 4, 40, 16, 128), BF),
             pltpu.VMEM((8, 4, 16, 128), BF),
             pltpu.VMEM((64, 16, 128), BF),
-            pltpu.SemaphoreType.DMA((100,)),
-            pltpu.SemaphoreType.DMA((100,)),
-            pltpu.SemaphoreType.DMA((64,)),
-        ],
-        compiler_params=pltpu.CompilerParams(collective_id=0, has_side_effects=True, vmem_limit_bytes=LIMIT),
-        name="gather",
-    )(block_slot, key_weight.reshape(4, 8, 16, 1024))
-
-
-def scatter_grads(owner, part, small):
-    return pl.pallas_call(
-        scatter_kernel,
-        out_shape=(
-            jax.ShapeDtypeStruct((4, 8, 16, 1024), F32),
-            jax.ShapeDtypeStruct((48, 128), F32),
-        ),
-        in_specs=[SM, ANY, VM],
-        out_specs=(VM, VM),
-        scratch_shapes=[
             pltpu.VMEM((4, 4, 4, 40, 16, 128), BF),
             pltpu.VMEM((4, 4, 4, 20, 16, 128), BF),
             pltpu.VMEM((64, 16, 128), BF),
@@ -482,40 +563,31 @@
             pltpu.VMEM((2, 4, 4, 8, 16, 128), BF),
             pltpu.VMEM((2, 48, 128), F32),
             pltpu.VMEM((3, 4, 48, 128), F32),
-            pltpu.SemaphoreType.DMA((130,)),
-            pltpu.SemaphoreType.DMA((130,)),
-            pltpu.SemaphoreType.DMA((64,)),
+            pltpu.VMEM((ROWS, WIDTH), BF),
+            pltpu.VMEM((ROWS, WIDTH), BF),
+            pltpu.VMEM((ROWS, KEYS), BF),
+            pltpu.VMEM((ROWS, KEYS), BF),
+            pltpu.VMEM((ROWS, 128), F32),
+            pltpu.VMEM((ROWS, 128), F32),
+            pltpu.VMEM((48, 128), F32),
+            pltpu.SemaphoreType.DMA((200,)),
+            pltpu.SemaphoreType.DMA((200,)),
+            pltpu.SemaphoreType.DMA((40,)),
         ] + scatter_scratch(),
-        compiler_params=pltpu.CompilerParams(collective_id=1, has_side_effects=True, vmem_limit_bytes=LIMIT),
-        name="scatter",
-    )(owner, part.reshape(40, 8, 16, 1024), small)
+        compiler_params=pltpu.CompilerParams(collective_id=0, has_side_effects=True, vmem_limit_bytes=LIMIT),
+        name="fused",
+    )(block_slot, owner, tokens, gain, bias, key_weight, cotangent)
 
 
 def local(tokens, norm_gain, key_bias, key_weight, cotangent, block_slot):
-    row_count, width = tokens.shape
-    grad_scale = float(row_count * lax.axis_size("shard") * lax.axis_size("rep")) ** (-0.5)
     slots = jnp.arange(64, dtype=jnp.int32)
     hit = block_slot[None, :] == slots[:, None]
     owner = jnp.max(jnp.where(hit, jnp.arange(40, dtype=jnp.int32)[None, :], -1), axis=1)
-    weight = gather_weights(block_slot, key_weight).reshape(width, 1024)
-    values = tokens.astype(F32)
-    inv_rms = lax.rsqrt(jnp.mean(values * values, axis=-1, keepdims=True) + EPS)
-    normed = (values * inv_rms * norm_gain).astype(BF)
-    forward = jnp.dot(normed, weight, preferred_element_type=F32)
-    projected = (forward + key_bias).astype(BF)
-    grad_normed = lax.dot_general(cotangent, weight, (((1,), (1,)), ((), ())), preferred_element_type=F32)
-    scaled = grad_normed * norm_gain
-    inner = jnp.mean(scaled * values, axis=-1, keepdims=True)
-    token_grad = (inv_rms * (scaled - values * inv_rms * inv_rms * inner)).astype(BF)
-    part = (
-        lax.dot_general(normed, cotangent, (((0,), (0,)), ((), ())), preferred_element_type=F32) * grad_scale
-    ).astype(BF)
-    gain_part = jnp.sum(grad_normed * values * inv_rms, axis=0) * grad_scale
-    bias_part = jnp.sum(cotangent.astype(F32), axis=0) * grad_scale
-    small = jnp.concatenate([gain_part, bias_part]).reshape(48, 128)
-    sums, total = scatter_grads(owner, part, small)
+    projected, token_grad, slab, total = fused(
+        block_slot, owner, tokens, norm_gain.reshape(1, WIDTH), key_bias.reshape(1, KEYS),
+        key_weight.reshape(4, 8, 16, KEYS), cotangent)
     total = total.reshape(-1)
-    return (projected, token_grad, sums.reshape(512, 1024), total[:width], total[width:])
+    return (projected, token_grad, slab.reshape(512, KEYS).astype(F32), total[:WIDTH], total[WIDTH:])
 
 
 def solution(mesh):

time: 181 us -> 126 us (0.70)
  matrix products: 27.7 us -> 0 us
  local copies, waits for them, and re-layouts: 18.4 us -> 6.75 us
  Pallas kernels: 125 us -> 114 us
  other arithmetic: 8.49 us -> 4.04 us
    dot_general x3 -> x0, matrix products: 27.7 us -> none  [the longest x1 10.5 us: local(): forward = jnp.dot(normed, weight, preferred_element_type=F32)]
    unnamed x19 -> x4, local copies, waits for them, and re-layouts: 15.8 us -> 3.99 us
    pallas_call x2 -> x1, Pallas kernels: 125 us -> 114 us  [fused(): pl.pallas_call(fused_kernel, out_shape=(jax.ShapeDtypeStruct((ROWS, KEYS)...]
    reduce_sum x2 -> x0, other arithmetic: 3.32 us -> none  [the longest x1 3.18 us: local(): inv_rms = lax.rsqrt(jnp.mean(values * values, axis=-1, keepdims=True) + EPS)]
where the time goes in v2:
time: 126 us
  Pallas kernels  114 us (90%)
  local copies, waits for them, and re-layouts  6.75 us (5%)
  other arithmetic  4.04 us (3%)
    pallas_call x1, Pallas kernels, fused(): pl.pallas_call(fused_kernel, out_shape=(jax.ShapeDtypeStruct((ROWS, KEYS)...  114 us
    unnamed x4, local copies, waits for them, and re-layouts  3.99 us
    convert_element_type x1, other arithmetic, local(): slab.reshape(512, KEYS).astype(F32)  2.79 us

profile of v2, /device:TPU:0, one launch (start us, length us, event | category | flops | bytes accessed | tf_op | source)
XLA Modules:
  0.0 125.6 jit_solution(1887949993557854477)
XLA Ops:
  0.6 1.3 select_reduce_fusion.owner_ref
  1.9 114.2 %fused.1 = (bf16[384,1024]{1,0:T(8,128)(2,1)}, bf16[384,5120]{1,0:T(8,128)(2,1)}, bf16[4,8,16,1024]{3,2,1,0:T(8,128)(2,1)}, f32[48,128]{1,0:T(8,128)}) custom-call(s32[40]{0:T(128)} %slots_ref.1, s32[64]{0:T(128)} %select_reduce_fusion.owner_ref, bf16[384,5120]{1,0:T(8,128)(2,1)} %tok_ref.1, f32[1,5120]{1,0:T(1,128)} %bitcast.11, f32[1,1024]{1,0:T(1,128)} %bitcast.12, ...), custom_call_target="tpu_custom_call" | custom-call | tf_op jit(solution)/shard_map/fused/pallas_call | solution.py:545
  116.0 0.0 copy-start
  116.1 1.5 %slice_bitcast_fusion = f32[5120]{0:T(1024)} fusion(f32[48,128]{1,0:T(8,128)} %get-tuple-element.12), kind=kLoop, calls=%fused_computation.1 | loop fusion | bytes 40960 | tf_op jit(solution)/shard_map/slice | solution.py:590
  117.5 1.3 %slice_bitcast_fusion.1 = f32[1024]{0:T(1024)} fusion(f32[48,128]{1,0:T(8,128)} %get-tuple-element.12), kind=kLoop, calls=%fused_computation.4 | loop fusion | bytes 8192 | tf_op jit(solution)/shard_map/slice | solution.py:590
  118.8 2.8 %bitcast_convert_fusion = f32[512,1024]{1,0:T(8,128)} fusion(bf16[4,8,16,1024]{3,2,1,0:T(8,128)(2,1)} %get-tuple-element.11), kind=kLoop, calls=%fused_computation | loop fusion | flops 524288 | bytes 3145728 | tf_op jit(solution)/shard_map/convert_element_type | solution.py:590
  121.6 2.1 %copy.13 = bf16[384,1024]{1,0:T(8,128)(2,1)} copy(bf16[384,1024]{1,0:T(8,128)(2,1)} %get-tuple-element.18) | data formatting | bytes 1572864
  123.7 0.0 copy-done
  123.7 1.9 %copy.14 = bf16[384,5120]{1,0:T(8,128)(2,1)} copy(bf16[384,5120]{1,0:T(8,128)(2,1)S(1)} %copy-done) | data formatting | bytes 7864320
Async XLA Ops:
  116.0 7.6 %copy-start = (bf16[384,5120]{1,0:T(8,128)(2,1)S(1)}, bf16[384,5120]{1,0:T(8,128)(2,1)}, u32[]{:S(2)}) copy-start(bf16[384,5120]{1,0:T(8,128)(2,1)} %get-tuple-element.19) | copy-start | bytes 11796484

commit v3 on v2

v3 whole, which is shorter than its diff:
```python
import functools

import jax
import jax.numpy as jnp
from jax import lax
from jax.experimental import pallas as pl
from jax.experimental.pallas import tpu as pltpu
from jax.sharding import PartitionSpec as P

MESH = pl.DeviceIdType.MESH
BLK = 128
EPS = 1e-06
HALF = 20
PARTS = (
    (0, 7, 4, (0, 1, 2)),
    (7, 7, 3, (1, 2, 0)),
    (14, 6, 3, (2, 0, 1)),
)
BF = jnp.bfloat16
F32 = jnp.float32


class Place:
    def __init__(self):
        big = lax.axis_index("shard")
        rep = lax.axis_index("rep")
        self.big, self.rep = big, rep
        self.c = lax.rem(big, 2)
        self.s = lax.div(big, 2)
        self.z = lax.rem(self.s, 4)
        xh = lax.div(big, 8)
        xl = lax.div(rep, 4)
        self.xl = xl
        self.xh = xh
        self.pi = lax.rem(xl + xh, 2)
        self.x = xh * 2 + xl
        self.y = lax.rem(rep, 4)
        self.pos = (self.x, self.y, self.z)

    def at(self, axis, step):
        return lax.rem(self.pos[axis] + step, 4)

    def device(self, pos, c):
        x, y, z = pos
        big = (lax.div(x, 2) * 4 + z) * 2 + c
        return (big, lax.rem(x, 2) * 4 + y)

    def ring(self, axis, step):
        pos = list(self.pos)
        pos[axis] = self.at(axis, step)
        return self.device(pos, self.c)

    def partner(self):
        return (self.s * 2 + 1 - self.c, self.rep)

    def x_pair(self):
        return (self.big, (1 - self.xl) * 4 + self.y)

    def group(self):
        for i in range(2):
            for j in range(4):
                for d in range(2):
                    if i == j == d == 0:
                        continue
                    xh = self.xh if i == 0 else 1 - self.xh
                    xl = self.xl if i == 0 else 1 - self.xl
                    core = self.c if d == 0 else 1 - self.c
                    yield i, j, d, ((xh * 4 + self.at(2, j)) * 2 + core, xl * 4 + self.y)


class Wires:
    def __init__(self, send, recv, limit):
        self.send, self.recv, self.limit, self.n, self.open = send, recv, limit, 0, []

    def put(self, src, dst, device):
        i = self.n
        self.n += 1
        assert i < self.limit, "sems"
        copy = pltpu.make_async_remote_copy(
            src_ref=src, dst_ref=dst, send_sem=self.send.at[i], recv_sem=self.recv.at[i],
            device_id=device, device_id_type=MESH,
        )
        copy.start()
        self.open.append(copy)
        return copy

    def drain(self):
        for copy in self.open:
            copy.wait_send()
        self.open = []


def greet(place):
    barrier = pltpu.get_barrier_semaphore()
    peers = [device for _, _, _, device in place.group()]
    peers += [place.x_pair(), place.ring(0, 2)]
    peers += [place.ring(1, step) for step in (1, 2, 3)]
    for device in peers:
        pl.semaphore_signal(barrier, inc=1, device_id=device, device_id_type=MESH)
    return lambda: pl.semaphore_wait(barrier, len(peers))


def locate(place, order, k, v, done, later):
    out = [None] * 3
    for j, axis in enumerate(order):
        out[axis] = v if j == k else (done(axis) if j < k else later(axis))
    return tuple(out)


class Gather:
    def __init__(self, place, wires, w):
        self.place, self.wires, self.w = place, wires, w
        self.base = place.c * HALF
        self.stage = {}
        self.passed = {}
        self.pair = []

    def view(self, p, k, v, first, count):
        off, nb, h, order = PARTS[p]
        pos = self.place.pos
        idx = locate(self.place, order, k, v, lambda a: slice(None), lambda a: pos[a])
        return self.w.at[idx + (pl.ds(self.base + off + first, count),)]

    def move(self, p, k, v, first, count, device):
        ref = self.view(p, k, v, first, count)
        return self.wires.put(ref, ref, device)

    def start(self, p, k, part=None):
        off, nb, h, order = PARTS[p]
        place, axis = self.place, order[k]
        me = place.pos[axis]
        up, down = place.ring(axis, 1), place.ring(axis, 3)
        if k == 0:
            self.stage[p, k] = [
                self.move(p, k, me, 0, nb, device) for device in (place.ring(axis, 2), up, down)]
            return
        if part != 1:
            u0 = self.move(p, k, me, 0, h, up)
            d1 = self.move(p, k, me, h, nb - h, down)
            self.stage[p, k] = [u0, d1]
        if part != 0:
            u1 = self.move(p, k, me, h, nb - h, up)
            d0 = self.move(p, k, me, 0, h, down)
            self.stage[p, k] += [u1, d0]

    def share(self, p, k, v, first, count):
        if k == 2:
            self.pair.append(self.move(p, k, v, first, count, self.place.partner()))

    def forward(self, p, k):
        off, nb, h, order = PARTS[p]
        place, axis = self.place, order[k]
        u0, d1 = self.stage[p, k][:2]
        below, above = place.at(axis, 3), place.at(axis, 1)
        u0.wait_recv()
        f0 = self.move(p, k, below, 0, h, place.ring(axis, 1))
        d1.wait_recv()
        f1 = self.move(p, k, above, h, nb - h, place.ring(axis, 3))
        self.share(p, k, below, 0, h)
        self.share(p, k, above, h, nb - h)
        self.passed[p, k] = [f0, f1]

    def finish(self, p, k):
        off, nb, h, order = PARTS[p]
        place, axis = self.place, order[k]
        if k == 0:
            for copy in self.stage[p, k]:
                copy.wait_recv()
            return
        u0, d1, u1, d0 = self.stage[p, k]
        f0, f1 = self.passed[p, k]
        below, above, across = place.at(axis, 3), place.at(axis, 1), place.at(axis, 2)
        u1.wait_recv()
        self.share(p, k, below, h, nb - h)
        d0.wait_recv()
        self.share(p, k, above, 0, h)
        f0.wait_recv()
        self.share(p, k, across, 0, h)
        f1.wait_recv()
        self.share(p, k, across, h, nb - h)
        if k == 1:
            self.share(p, 2, place.pos[order[2]], 0, nb)


def rest_of(t, count):
    if count == 2:
        return (lax.div(t, 4), lax.rem(t, 4))
    return (t,) if count == 1 else ()


class Scatter:
    def __init__(self, place, wires, g, bufs):
        self.place, self.wires, self.g, self.bufs = place, wires, g, bufs
        self.base = place.c * HALF
        self.stage = {}
        self.passed = {}

    def index(self, p, k, v, later):
        order = PARTS[p][3]
        pos = self.place.pos
        return locate(self.place, order, k, v, lambda a: pos[a], later)

    def view(self, p, k, v, first, count):
        idx = self.index(p, k, v, lambda a: slice(None))
        return self.g.at[idx + (pl.ds(self.base + PARTS[p][0] + first, count),)]

    def tile(self, p, k, v, rest, first, count):
        order = PARTS[p][3]
        later = sorted(order[k + 1:])
        idx = self.index(p, k, v, lambda a: rest[later.index(a)])
        return idx + (pl.ds(self.base + PARTS[p][0] + first, count),)

    def buf(self, p, k, which):
        return self.bufs[p][k][which]

    def start(self, p, k, part=None):
        off, nb, h, order = PARTS[p]
        place, axis = self.place, order[k]
        put, full = self.wires.put, (slice(None),) * (2 - k)
        up, down = place.ring(axis, 1), place.ring(axis, 3)
        over, under = place.at(axis, 1), place.at(axis, 3)
        across = place.at(axis, 2)
        ta, tb, fm, fp = self.bufs[p][k]
        if k == 2:
            self.stage[p, k] = [
                put(self.view(p, k, across, 0, nb), ta, place.ring(axis, 2)),
                put(self.view(p, k, over, 0, nb), fm, up),
                put(self.view(p, k, under, 0, nb), fp, down)]
            return
        if part != 1:
            a = put(self.view(p, k, across, 0, h), ta, up)
            b = put(self.view(p, k, across, h, nb - h), tb, down)
            self.stage[p, k] = [a, b]
        if part != 0:
            u = put(self.view(p, k, over, h, nb - h), fm.at[full + (pl.ds(h, nb - h),)], up)
            d = put(self.view(p, k, under, 0, h), fp.at[full + (pl.ds(0, h),)], down)
            self.stage[p, k] += [u, d]

    def forward(self, p, k):
        off, nb, h, order = PARTS[p]
        place, axis = self.place, order[k]
        put, full = self.wires.put, (slice(None),) * (2 - k)
        up, down = place.ring(axis, 1), place.ring(axis, 3)
        over, under = place.at(axis, 1), place.at(axis, 3)
        ta, tb, fm, fp = self.bufs[p][k]
        a, b = self.stage[p, k][:2]
        g = self.g

        def add(t, v, buf, first, count):
            rest = rest_of(t, 2 - k)
            idx = self.tile(p, k, v, rest, first, count)
            g[idx] = g[idx] + buf[rest]

        a.wait_recv()
        pl.loop(0, 4 ** (2 - k))(lambda t: add(t, over, ta, 0, h))
        fa = put(self.view(p, k, over, 0, h), fm.at[full + (pl.ds(0, h),)], up)
        b.wait_recv()
        pl.loop(0, 4 ** (2 - k))(lambda t: add(t, under, tb, h, nb - h))
        fb = put(self.view(p, k, under, h, nb - h), fp.at[full + (pl.ds(h, nb - h),)], down)
        self.passed[p, k] = [fa, fb]

    def finish(self, p, k):
        off, nb, h, order = PARTS[p]
        me = self.place.pos[order[k]]
        ta, tb, fm, fp = self.bufs[p][k]
        g = self.g
        if k == 2:
            for copy in self.stage[p, k]:
                copy.wait_recv()
            idx = self.tile(p, k, me, (), 0, nb)
            total = (g[idx].astype(F32) + ta[...].astype(F32)) + (fm[...].astype(F32) + fp[...].astype(F32))
            g[idx] = total.astype(BF)
            return
        for copy in self.stage[p, k][2:] + self.passed[p, k]:
            copy.wait_recv()

        def add(t):
            rest = rest_of(t, 2 - k)
            idx = self.tile(p, k, me, rest, 0, nb)
            total = g[idx].astype(F32) + fm[rest].astype(F32) + fp[rest].astype(F32)
            g[idx] = total.astype(BF)

        pl.loop(0, 4 ** (2 - k))(add)


def scatter_scratch():
    out = []
    for p in range(3):
        _, nb, h, _ = PARTS[p]
        for k in range(3):
            lead = (4,) * (2 - k)
            sizes = (nb, 1, nb, nb) if k == 2 else (h, nb - h, nb, nb)
            out += [pltpu.VMEM(lead + (n, 16, 128), BF) for n in sizes]
    return out


def scatter_bufs(flat):
    return [[flat[(p * 3 + k) * 4:(p * 3 + k) * 4 + 4] for k in range(3)] for p in range(3)]


class Small:
    def __init__(self, place, wires, first, rest):
        self.place, self.wires, self.first, self.rest = place, wires, first, rest
        self.sent = []

    def start(self, k, value):
        place = self.place
        if k == 0:
            self.first[place.c] = value
            own = self.first.at[place.c]
            self.sent = [self.wires.put(own, own, place.partner())]
            return
        axis = k - 1
        self.rest[axis, place.pos[axis]] = value
        own = self.rest.at[axis, place.pos[axis]]
        self.sent = [self.wires.put(own, own, place.ring(axis, step)) for step in (1, 3, 2)]

    def finish(self, k):
        for copy in self.sent:
            copy.wait_recv()
        if k == 0:
            return self.first[0] + self.first[1]
        t = self.rest
        return (t[k - 1, 0] + t[k - 1, 1]) + (t[k - 1, 2] + t[k - 1, 3])


WIDTH = 5120
KEYS = 1024
ROWS = 384


def fused_kernel(slots_ref, owner_ref, tok_ref, gain_ref, bias_ref, kw_ref, cot_ref,
                 proj, grad_out, slab_out, gain_out, bias_out,
                 w, kws, held, g, half, slot, seen, fin, first, rest,
                 tok, normed, cot, inv, coef, small_v, even, odd, send, recv, local, *flat):
    place = Place()
    wires = Wires(send, recv, 220)
    grad_scale = float(ROWS * 128) ** (-0.5)
    loads = []

    def load(src, dst):
        copy = pltpu.make_async_copy(src, dst, local.at[len(loads)])
        copy.start()
        loads.append(copy)
        return copy

    wait_greet = greet(place)
    slabs = []
    for i in range(2):
        xh = place.xh if i == 0 else 1 - place.xh
        xl = place.xl if i == 0 else 1 - place.xl
        for t in range(4):
            col = pl.ds(pl.multiple_of((xh * 4 + t) * 128, 128), 128)
            slabs.append(load(kw_ref.at[:, xl * 4 + place.y, :, col], kws.at[i, t]))
    rows = [load(tok_ref.at[pl.ds(i * 64, 64)], tok.at[pl.ds(i * 64, 64)]) for i in range(6)]
    cots = load(cot_ref, cot)

    def norm(i):
        rows[i].wait()

        @pl.loop(i * 4, i * 4 + 4)
        def _(t):
            r = pl.ds(pl.multiple_of(t * 16, 16), 16)
            acc = [jnp.zeros((16, 128), F32)] * 4
            for j in range(40):
                v = tok[r, j * 128:(j + 1) * 128].astype(F32)
                acc[j % 4] = acc[j % 4] + v * v
            total = jnp.sum((acc[0] + acc[1]) + (acc[2] + acc[3]), axis=1, keepdims=True)
            scale = jnp.broadcast_to(lax.rsqrt(total * (1.0 / WIDTH) + EPS), (16, 128))
            inv[r, :] = scale
            for j in range(40):
                col = slice(j * 128, (j + 1) * 128)
                normed[r, col] = (tok[r, col].astype(F32) * scale * gain_ref[:, col]).astype(BF)

    own = place.c * HALF
    other = (1 - place.c) * HALF
    full = (slice(None),) * 3

    def blocks(side, first, count, add):
        b = side + first
        left = normed[:, pl.ds(pl.multiple_of(b * 128, 128), count * 128)]
        value = lax.dot_general(left, cot[...], (((0,), (0,)), ((), ())), preferred_element_type=F32)
        value = value * grad_scale
        for i in range(count):
            for r in range(8):
                for q in range(8):
                    at = (q // 4 * 2 + r // 4, r % 4, q % 4)
                    tile = value[i * 128 + r * 16:i * 128 + r * 16 + 16, q * 128:(q + 1) * 128]
                    if add:
                        tile = tile + half[at + (first + i,)].astype(F32)
                    g[at + (b + i,)] = tile.astype(BF)

    def partial(p, mine):
        off, nb = PARTS[p][:2]
        side = own if mine else other
        if mine:
            swap[p].wait_recv()

        @pl.loop(0, nb // 2)
        def _(t):
            blocks(side, off + 2 * t, 2, mine)

        if nb % 2:
            blocks(side, off + nb - 1, 1, mine)
        if not mine:
            swap.append(wires.put(
                g.at[full + (pl.ds(other + off, nb),)], half.at[full + (pl.ds(off, nb),)], place.partner()))

    swap = []
    gather = Gather(place, wires, w)
    scatter = Scatter(place, wires, g, scatter_bufs(flat))
    small = Small(place, wires, first, rest)
    come = []

    def trade_weights():
        for copy in slabs:
            copy.wait()
        mine = held.at[pl.ds(place.big * 4, 4)]
        for i, j, _, device in place.group():
            come.append(wires.put(kws.at[i, place.at(2, j)], mine, device))
        held[pl.ds(place.big * 4, 4)] = kws[0, place.z]

    def pick():
        for copy in come:
            copy.wait_recv()

        @pl.loop(0, HALF)
        def _(t):
            b = own + t
            w[place.x, place.y, place.z, b] = held[slots_ref[b]]

    def bias_sum():
        for j in range(8):
            small_v[40 + j:41 + j, :] = jnp.sum(
                cot[:, j * 128:(j + 1) * 128].astype(F32), axis=0, keepdims=True) * grad_scale

    def forward():
        for copy in gather.pair:
            copy.wait_recv()
        coef[...] = jnp.zeros_like(coef)

        @pl.loop(0, 4)
        def _(n):
            q = 2 * n
            x0, z0 = lax.div(q, 4) * 2, lax.rem(q, 4)
            right = jnp.concatenate(
                [jnp.concatenate([w[x0 + r // 4, r % 4, z0, b], w[x0 + r // 4, r % 4, z0 + 1, b]], axis=1)
                 for b in range(40) for r in range(8)], axis=0)
            value = jnp.dot(normed[...], right, preferred_element_type=F32)
            col = pl.ds(pl.multiple_of(n * 256, 256), 256)
            proj[:, col] = (value + bias_ref[:, col]).astype(BF)
            both = value * cot[:, col].astype(F32)
            coef[...] += both[:, :128] + both[:, 128:]

        coef[...] = jnp.broadcast_to(
            jnp.sum(coef[...], axis=1, keepdims=True), (ROWS, 128)) * inv[...] * (1.0 / WIDTH)

    def product(t, into):
        b = 2 * t
        right = jnp.concatenate(
            [jnp.concatenate([w[q // 4 * 2 + r // 4, r % 4, q % 4, b + i] for q in range(8)], axis=1)
             for i in range(2) for r in range(8)], axis=0)
        into[...] = lax.dot_general(cot[...], right, (((1,), (1,)), ((), ())), preferred_element_type=F32)

    def apply(t, grad):
        b = 2 * t
        for i in range(2):
            col = pl.ds(pl.multiple_of((b + i) * 128, 128), 128)
            gn = grad[:, i * 128:(i + 1) * 128]
            scale = inv[...]
            unit = tok[:, col].astype(F32) * scale
            small_v[pl.ds(b + i, 1), :] = jnp.sum(gn * unit, axis=0, keepdims=True) * grad_scale
            grad_out[:, col] = (gn * gain_ref[:, col] * scale - unit * coef[...]).astype(BF)

    def backward(low, high):
        if low == 0:
            product(0, even)

        @pl.loop(low, min(high, 9))
        def _(u):
            product(2 * u + 1, odd)
            apply(2 * u, even)
            product(2 * u + 2, even)
            apply(2 * u + 1, odd)

        if high == 10:
            product(19, odd)
            apply(18, even)
            apply(19, odd)

    def each(step, k, *part):
        for p in range(3):
            step(p, k, *part)

    def small_next(k):
        small.start(k + 1, small.finish(k))

    def small_end():
        total = small.finish(3)
        gain_out[...] = total[:40]
        bias_out[...] = total[40:]

    back = []

    def trade_grads():
        @pl.loop(0, 64)
        def _(t):
            b = owner_ref[t]
            ours = jnp.logical_and(b >= own, b < own + HALF)
            value = g[place.x, place.y, place.z, jnp.maximum(b, 0)]
            slot[t] = jnp.where(ours, value, jnp.zeros_like(value))

        for _, _, _, device in place.group():
            back.append(wires.put(
                slot.at[pl.ds(device[0] * 4, 4)], seen.at[place.c, place.xh, place.z], device))
        seen[place.c, place.xh, place.z] = slot[pl.ds(place.big * 4, 4)]

    pi, y = place.pi, place.y
    yup, ydown = place.ring(1, 1), place.ring(1, 3)
    below, above, across = place.at(1, 3), place.at(1, 1), place.at(1, 2)
    sent = {}

    def move(name, side, row, slot0, count, device):
        ref = fin.at[side, row, pl.ds(slot0, count)]
        sent[name] = wires.put(ref, ref, device)

    def ring(name, side, slot0):
        move(name + "u0", side, y, slot0, 1, yup)
        move(name + "d1", side, y, slot0 + 1, 1, ydown)
        move(name + "u1", side, y, slot0 + 1, 1, yup)
        move(name + "d0", side, y, slot0, 1, ydown)

    def ring_on(name, side, slot0):
        sent[name + "u0"].wait_recv()
        move(name + "f0", side, below, slot0, 1, yup)
        sent[name + "d1"].wait_recv()
        move(name + "f1", side, above, slot0 + 1, 1, ydown)

    def spread_start():
        for copy in back:
            copy.wait_recv()
        for q in range(8):
            fin[pi, y, :, q // 4, q % 4] = seen[0, q // 4, q % 4] + seen[1, q // 4, q % 4]
        move("px", pi, y, 0, 2, place.x_pair())
        ring("a", pi, 0)
        move("qx", pi, y, 2, 2, place.x_pair())
        ring("c", pi, 2)

    def spread_middle():
        sent["px"].wait_recv()
        ring("b", 1 - pi, 0)
        ring_on("a", pi, 0)
        ring_on("c", pi, 2)
        sent["cu1"].wait_recv()
        move("rx", pi, below, 2, 2, place.x_pair())
        sent["cd0"].wait_recv()
        move("sx", pi, above, 2, 2, place.x_pair())

    def spread_end():
        sent["cf0"].wait_recv()
        sent["cf1"].wait_recv()
        move("tx", pi, across, 2, 2, place.x_pair())
        ring_on("b", 1 - pi, 0)
        for name in ("au1", "ad0", "af0", "af1", "bu1", "bd0", "bf0", "bf1", "qx", "rx", "sx", "tx"):
            sent[name].wait_recv()

        @pl.loop(0, 32)
        def _(t):
            i, r = lax.div(t, 8), lax.rem(t, 8)
            for q in range(8):
                side = lax.rem(lax.div(r, 4) + q // 4, 2)
                slab_out[i, r, :, q * 128:(q + 1) * 128] = fin[side, lax.rem(r, 4), i, q // 4, q % 4].astype(F32)

    for i in range(3): norm(i)
    wait_greet()
    trade_weights()
    for i in range(3, 6): norm(i)
    cots.wait()
    partial(0, False)
    partial(1, False)
    pick()
    each(gather.start, 0)
    partial(2, False)
    partial(0, True)
    each(gather.finish, 0)
    each(gather.start, 1)
    partial(1, True)
    partial(2, True)
    each(gather.forward, 1)
    each(scatter.start, 0, 0)
    bias_sum()
    each(gather.finish, 1)
    each(gather.start, 2)
    each(scatter.start, 0, 1)
    each(gather.forward, 2)
    each(scatter.forward, 0)
    each(gather.finish, 2)
    forward()
    each(scatter.finish, 0)
    each(scatter.start, 1)
    backward(0, 4)
    each(scatter.forward, 1)
    backward(4, 8)
    each(scatter.finish, 1)
    each(scatter.start, 2)
    backward(8, 10)
    small.start(0, small_v[...])
    small_next(0)
    each(scatter.finish, 2)
    trade_grads()
    small_next(1)
    spread_start()
    small_next(2)
    spread_middle()
    small_end()
    spread_end()
    wires.drain()


def emit_kernel(*refs):
    sem = refs[-1]
    copies = [pltpu.make_async_copy(refs[i], refs[5 + i], sem.at[i]) for i in range(5)]
    for copy in copies:
        copy.start()
    for copy in copies:
        copy.wait()


VM = pl.BlockSpec(memory_space=pltpu.VMEM)
SM = pl.BlockSpec(memory_space=pltpu.SMEM)
ANY = pl.BlockSpec(memory_space=pl.ANY)
LIMIT = 56 * 1024 * 1024


OUTS = (
    ((ROWS, KEYS), BF),
    ((ROWS, WIDTH), BF),
    ((4, 8, 16, KEYS), F32),
    ((40, 128), F32),
    ((8, 128), F32),
)


def fused(block_slot, owner, tokens, gain, bias, key_weight, cotangent):
    outs = pl.pallas_call(
        fused_kernel,
        out_shape=tuple(pltpu.VMEM(*out) for out in OUTS),
        in_specs=[SM, SM, ANY, VM, VM, ANY, ANY],
        out_specs=(VM,) * 5,
        scratch_shapes=[
            pltpu.VMEM((4, 4, 4, 40, 16, 128), BF),
            pltpu.VMEM((2, 4, 4, 16, 128), BF),
            pltpu.VMEM((64, 16, 128), BF),
            pltpu.VMEM((4, 4, 4, 40, 16, 128), BF),
            pltpu.VMEM((4, 4, 4, 20, 16, 128), BF),
            pltpu.VMEM((64, 16, 128), BF),
            pltpu.VMEM((2, 2, 4, 4, 16, 128), BF),
            pltpu.VMEM((2, 4, 4, 2, 4, 16, 128), BF),
            pltpu.VMEM((2, 48, 128), F32),
            pltpu.VMEM((3, 4, 48, 128), F32),
            pltpu.VMEM((ROWS, WIDTH), BF),
            pltpu.VMEM((ROWS, WIDTH), BF),
            pltpu.VMEM((ROWS, KEYS), BF),
            pltpu.VMEM((ROWS, 128), F32),
            pltpu.VMEM((ROWS, 128), F32),
            pltpu.VMEM((48, 128), F32),
            pltpu.VMEM((ROWS, 256), F32),
            pltpu.VMEM((ROWS, 256), F32),
            pltpu.SemaphoreType.DMA((220,)),
            pltpu.SemaphoreType.DMA((220,)),
            pltpu.SemaphoreType.DMA((40,)),
        ] + scatter_scratch(),
        compiler_params=pltpu.CompilerParams(collective_id=0, has_side_effects=True, vmem_limit_bytes=LIMIT),
        name="fused",
    )(block_slot, owner, tokens, gain, bias, key_weight, cotangent)
    return pl.pallas_call(
        emit_kernel,
        out_shape=tuple(jax.ShapeDtypeStruct(*out) for out in OUTS),
        in_specs=[VM] * 5,
        out_specs=(ANY,) * 5,
        scratch_shapes=[pltpu.SemaphoreType.DMA((5,))],
        compiler_params=pltpu.CompilerParams(vmem_limit_bytes=1024 * 1024),
        name="emit",
    )(*(pltpu.with_memory_space_constraint(out, pltpu.VMEM) for out in outs))


def local(tokens, norm_gain, key_bias, key_weight, cotangent, block_slot):
    slots = jnp.arange(64, dtype=jnp.int32)
    hit = block_slot[None, :] == slots[:, None]
    owner = jnp.max(jnp.where(hit, jnp.arange(40, dtype=jnp.int32)[None, :], -1), axis=1)
    projected, token_grad, slab, gain, bias = fused(
        block_slot, owner, tokens, norm_gain.reshape(1, WIDTH), key_bias.reshape(1, KEYS),
        key_weight.reshape(4, 8, 16, KEYS), cotangent)
    return (projected, token_grad, slab.reshape(512, KEYS), gain.reshape(-1), bias.reshape(-1))


def solution(mesh):
    return jax.shard_map(
        local,
        mesh=mesh,
        in_specs=(
            P(("shard", "rep"), None),
            P(),
            P(),
            P("shard", None),
            P(("shard", "rep"), None),
            P(),
        ),
        out_specs=(
            P(("shard", "rep"), None),
            P(("shard", "rep"), None),
            P("shard", None),
            P(),
            P(),
        ),
        check_vma=False,
    )
```

time: 126 us -> 100 us (0.79)
  Pallas kernels: 114 us -> 98.4 us
  local copies, waits for them, and re-layouts: 6.75 us -> 0 us
  other arithmetic: 4.04 us -> 1.26 us
    pallas_call x1 -> x2, Pallas kernels: 114 us -> 98.4 us  [the longest x1 95.4 us: fused(): pl.pallas_call(fused_kernel, out_shape=tuple((pltpu.VMEM(*out) for out in...]
    unnamed x4 -> x0, local copies, waits for them, and re-layouts: 3.99 us -> none
    convert_element_type x1 -> x0, other arithmetic: 2.79 us -> none  [local(): slab.reshape(512, KEYS).astype(F32)]
    slice x2 -> x0, local copies, waits for them, and re-layouts: 2.76 us -> none  [the longest x1 1.49 us: local(): total[:WIDTH]]
where the time goes in v3:
time: 100 us
  Pallas kernels  98.4 us (98%)
  other arithmetic  1.26 us (1%)
    pallas_call x1, Pallas kernels, fused(): pl.pallas_call(fused_kernel, out_shape=tuple((pltpu.VMEM(*out) for out in...  95.4 us
    pallas_call x1, Pallas kernels, fused(): pl.pallas_call(emit_kernel, out_shape=tuple((jax.ShapeDtypeStruct(*out) f...  2.92 us

profile of v3, /device:TPU:0, one launch (start us, length us, event | category | flops | bytes accessed | tf_op | source)
XLA Modules:
  0.0 100.3 jit_solution(10551025577152357570)
XLA Ops:
  0.6 1.3 %select_reduce_fusion.owner_ref = s32[64]{0:T(128)} fusion(s32[40]{0:T(128)} %slots_ref.1), kind=kLoop, calls=%fused_computation | loop fusion | flops 7616 | bytes 416 | tf_op jit(solution)/shard_map/reduce_max | solution.py:690
  1.9 95.4 %fused.1 = (bf16[384,1024]{1,0:T(8,128)(2,1)S(1)}, bf16[384,5120]{1,0:T(8,128)(2,1)S(1)}, f32[4,8,16,1024]{3,2,1,0:T(8,128)S(1)}, f32[40,128]{1,0:T(8,128)S(1)}, f32[8,128]{1,0:T(8,128)S(1)}) custom-call(s32[40]{0:T(128)} %slots_ref.1, s32[64]{0:T(128)} %select_reduce_fusion.owner_ref, bf16[384,5120]{1,0:T(8,128)(2,1)} %tok_ref.1, f32[1,5120]{1,0:T(1,128)} %bitcast.7, ...), custom_call_target="tpu_custom_call" | custom-call | tf_op jit(solution)/shard_map/fused/pallas_call | solution.py:645
  97.3 2.9 %emit.1 = (bf16[384,1024]{1,0:T(8,128)(2,1)}, bf16[384,5120]{1,0:T(8,128)(2,1)}, f32[4,8,16,1024]{3,2,1,0:T(8,128)}, f32[40,128]{1,0:T(8,128)}, f32[8,128]{1,0:T(8,128)}) custom-call(bf16[384,1024]{1,0:T(8,128)(2,1)S(1)} %get-tuple-element.15.refs_0_, bf16[384,5120]{1,0:T(8,128)(2,1)S(1)} %get-tuple-element.16.refs_1_, ...), custom_call_target="tpu_custom_call" | custom-call | tf_op jit(solution)/shard_map/emit/pallas_call | solution.py:676

commit v4 on v3

--- a/solution.py
+++ b/solution.py
@@ -70,24 +70,35 @@
 
 class Wires:
     def __init__(self, send, recv, limit):
-        self.send, self.recv, self.limit, self.n, self.open = send, recv, limit, 0, []
+        self.send, self.recv, self.limit, self.groups = send, recv, limit, []
+
+    def group(self, total):
+        i = len(self.groups)
+        assert i < self.limit, "sems"
+        self.groups.append(Group(self.send.at[i], self.recv.at[i], total))
+        return self.groups[-1]
 
     def put(self, src, dst, device):
-        i = self.n
-        self.n += 1
-        assert i < self.limit, "sems"
-        copy = pltpu.make_async_remote_copy(
-            src_ref=src, dst_ref=dst, send_sem=self.send.at[i], recv_sem=self.recv.at[i],
+        return self.group(dst).put(src, dst, device)
+
+    def drain(self):
+        for group in self.groups:
+            pltpu.make_async_copy(group.total, group.total, group.send).wait()
+
+
+class Group:
+    def __init__(self, send, recv, total):
+        self.send, self.recv, self.total = send, recv, total
+
+    def put(self, src, dst, device):
+        pltpu.make_async_remote_copy(
+            src_ref=src, dst_ref=dst, send_sem=self.send, recv_sem=self.recv,
             device_id=device, device_id_type=MESH,
-        )
-        copy.start()
-        self.open.append(copy)
-        return copy
-
-    def drain(self):
-        for copy in self.open:
-            copy.wait_send()
-        self.open = []
+        ).start()
+        return self
+
+    def wait(self):
+        pltpu.make_async_copy(self.total, self.total, self.recv).wait()
 
 
 def greet(place):
@@ -112,8 +123,7 @@
         self.place, self.wires, self.w = place, wires, w
         self.base = place.c * HALF
         self.stage = {}
-        self.passed = {}
-        self.pair = []
+        self.pair = wires.group(w.at[:, :, :, pl.ds(0, HALF)])
 
     def view(self, p, k, v, first, count):
         off, nb, h, order = PARTS[p]
@@ -121,62 +131,66 @@
         idx = locate(self.place, order, k, v, lambda a: slice(None), lambda a: pos[a])
         return self.w.at[idx + (pl.ds(self.base + off + first, count),)]
 
-    def move(self, p, k, v, first, count, device):
+    def move(self, group, p, k, v, first, count, device):
         ref = self.view(p, k, v, first, count)
-        return self.wires.put(ref, ref, device)
+        (group or self.wires.group(ref)).put(ref, ref, device)
+        return group or self.wires.groups[-1]
 
     def start(self, p, k, part=None):
         off, nb, h, order = PARTS[p]
-        place, axis = self.place, order[k]
+        place, axis, group = self.place, order[k], self.wires.group
         me = place.pos[axis]
         up, down = place.ring(axis, 1), place.ring(axis, 3)
         if k == 0:
-            self.stage[p, k] = [
-                self.move(p, k, me, 0, nb, device) for device in (place.ring(axis, 2), up, down)]
+            both = group(self.w.at[0, 0, 0, pl.ds(0, 3 * nb)])
+            for device in (place.ring(axis, 2), up, down):
+                self.move(both, p, k, me, 0, nb, device)
+            self.stage[p, k] = both
             return
         if part != 1:
-            u0 = self.move(p, k, me, 0, h, up)
-            d1 = self.move(p, k, me, h, nb - h, down)
+            u0 = self.move(None, p, k, me, 0, h, up)
+            d1 = self.move(None, p, k, me, h, nb - h, down)
             self.stage[p, k] = [u0, d1]
         if part != 0:
-            u1 = self.move(p, k, me, h, nb - h, up)
-            d0 = self.move(p, k, me, 0, h, down)
-            self.stage[p, k] += [u1, d0]
+            one = self.w.at[0, :, :, pl.ds(0, nb)]
+            two = self.w.at[0, pl.ds(0, 2), :, pl.ds(0, nb)]
+            late = group(one if k == 2 else two)
+            self.move(late, p, k, me, h, nb - h, up)
+            self.move(late, p, k, me, 0, h, down)
+            self.stage[p, k] += [late, group(one) if k == 2 else late]
 
     def share(self, p, k, v, first, count):
         if k == 2:
-            self.pair.append(self.move(p, k, v, first, count, self.place.partner()))
+            self.move(self.pair, p, k, v, first, count, self.place.partner())
 
     def forward(self, p, k):
         off, nb, h, order = PARTS[p]
         place, axis = self.place, order[k]
-        u0, d1 = self.stage[p, k][:2]
+        u0, d1, late, last = self.stage[p, k]
         below, above = place.at(axis, 3), place.at(axis, 1)
-        u0.wait_recv()
-        f0 = self.move(p, k, below, 0, h, place.ring(axis, 1))
-        d1.wait_recv()
-        f1 = self.move(p, k, above, h, nb - h, place.ring(axis, 3))
+        u0.wait()
+        self.move(last, p, k, below, 0, h, place.ring(axis, 1))
+        d1.wait()
+        self.move(last, p, k, above, h, nb - h, place.ring(axis, 3))
         self.share(p, k, below, 0, h)
         self.share(p, k, above, h, nb - h)
-        self.passed[p, k] = [f0, f1]
+
+    def arrive(self, p, k):
+        off, nb, h, order = PARTS[p]
+        place, axis = self.place, order[k]
+        self.stage[p, k][2].wait()
+        self.share(p, k, place.at(axis, 3), h, nb - h)
+        self.share(p, k, place.at(axis, 1), 0, h)
 
     def finish(self, p, k):
         off, nb, h, order = PARTS[p]
         place, axis = self.place, order[k]
         if k == 0:
-            for copy in self.stage[p, k]:
-                copy.wait_recv()
+            self.stage[p, k].wait()
             return
-        u0, d1, u1, d0 = self.stage[p, k]
-        f0, f1 = self.passed[p, k]
-        below, above, across = place.at(axis, 3), place.at(axis, 1), place.at(axis, 2)
-        u1.wait_recv()
-        self.share(p, k, below, h, nb - h)
-        d0.wait_recv()
-        self.share(p, k, above, 0, h)
-        f0.wait_recv()
+        self.stage[p, k][3].wait()
+        across = place.at(axis, 2)
         self.share(p, k, across, 0, h)
-        f1.wait_recv()
         self.share(p, k, across, h, nb - h)
         if k == 1:
             self.share(p, 2, place.pos[order[2]], 0, nb)
@@ -193,7 +207,6 @@
         self.place, self.wires, self.g, self.bufs = place, wires, g, bufs
         self.base = place.c * HALF
         self.stage = {}
-        self.passed = {}
 
     def index(self, p, k, v, later):
         order = PARTS[p][3]
@@ -222,28 +235,30 @@
         across = place.at(axis, 2)
         ta, tb, fm, fp = self.bufs[p][k]
         if k == 2:
-            self.stage[p, k] = [
-                put(self.view(p, k, across, 0, nb), ta, place.ring(axis, 2)),
-                put(self.view(p, k, over, 0, nb), fm, up),
-                put(self.view(p, k, under, 0, nb), fp, down)]
+            both = self.wires.group(self.g.at[0, 0, 0, pl.ds(0, 3 * nb)])
+            both.put(self.view(p, k, across, 0, nb), ta, place.ring(axis, 2))
+            both.put(self.view(p, k, over, 0, nb), fm, up)
+            both.put(self.view(p, k, under, 0, nb), fp, down)
+            self.stage[p, k] = both
             return
         if part != 1:
             a = put(self.view(p, k, across, 0, h), ta, up)
             b = put(self.view(p, k, across, h, nb - h), tb, down)
-            self.stage[p, k] = [a, b]
+            lead = (pl.ds(0, 2), slice(None), slice(None)) if k == 0 else (0, pl.ds(0, 2), slice(None))
+            self.stage[p, k] = [a, b, self.wires.group(self.g.at[lead + (pl.ds(0, nb),)])]
         if part != 0:
-            u = put(self.view(p, k, over, h, nb - h), fm.at[full + (pl.ds(h, nb - h),)], up)
-            d = put(self.view(p, k, under, 0, h), fp.at[full + (pl.ds(0, h),)], down)
-            self.stage[p, k] += [u, d]
+            rest = self.stage[p, k][2]
+            rest.put(self.view(p, k, over, h, nb - h), fm.at[full + (pl.ds(h, nb - h),)], up)
+            rest.put(self.view(p, k, under, 0, h), fp.at[full + (pl.ds(0, h),)], down)
 
     def forward(self, p, k):
         off, nb, h, order = PARTS[p]
         place, axis = self.place, order[k]
-        put, full = self.wires.put, (slice(None),) * (2 - k)
+        full = (slice(None),) * (2 - k)
         up, down = place.ring(axis, 1), place.ring(axis, 3)
         over, under = place.at(axis, 1), place.at(axis, 3)
         ta, tb, fm, fp = self.bufs[p][k]
-        a, b = self.stage[p, k][:2]
+        a, b, last = self.stage[p, k]
         g = self.g
 
         def add(t, v, buf, first, count):
@@ -251,13 +266,12 @@
             idx = self.tile(p, k, v, rest, first, count)
             g[idx] = g[idx] + buf[rest]
 
-        a.wait_recv()
+        a.wait()
         pl.loop(0, 4 ** (2 - k))(lambda t: add(t, over, ta, 0, h))
-        fa = put(self.view(p, k, over, 0, h), fm.at[full + (pl.ds(0, h),)], up)
-        b.wait_recv()
+        last.put(self.view(p, k, over, 0, h), fm.at[full + (pl.ds(0, h),)], up)
+        b.wait()
         pl.loop(0, 4 ** (2 - k))(lambda t: add(t, under, tb, h, nb - h))
-        fb = put(self.view(p, k, under, h, nb - h), fp.at[full + (pl.ds(h, nb - h),)], down)
-        self.passed[p, k] = [fa, fb]
+        last.put(self.view(p, k, under, h, nb - h), fp.at[full + (pl.ds(h, nb - h),)], down)
 
     def finish(self, p, k):
         off, nb, h, order = PARTS[p]
@@ -265,14 +279,12 @@
         ta, tb, fm, fp = self.bufs[p][k]
         g = self.g
         if k == 2:
-            for copy in self.stage[p, k]:
-                copy.wait_recv()
+            self.stage[p, k].wait()
             idx = self.tile(p, k, me, (), 0, nb)
             total = (g[idx].astype(F32) + ta[...].astype(F32)) + (fm[...].astype(F32) + fp[...].astype(F32))
             g[idx] = total.astype(BF)
             return
-        for copy in self.stage[p, k][2:] + self.passed[p, k]:
-            copy.wait_recv()
+        self.stage[p, k][2].wait()
 
         def add(t):
             rest = rest_of(t, 2 - k)
@@ -308,16 +320,17 @@
         if k == 0:
             self.first[place.c] = value
             own = self.first.at[place.c]
-            self.sent = [self.wires.put(own, own, place.partner())]
+            self.sent = self.wires.put(own, own, place.partner())
             return
         axis = k - 1
         self.rest[axis, place.pos[axis]] = value
         own = self.rest.at[axis, place.pos[axis]]
-        self.sent = [self.wires.put(own, own, place.ring(axis, step)) for step in (1, 3, 2)]
+        self.sent = self.wires.group(self.rest.at[0, pl.ds(0, 3)])
+        for step in (2, 1, 3):
+            self.sent.put(own, own, place.ring(axis, step))
 
     def finish(self, k):
-        for copy in self.sent:
-            copy.wait_recv()
+        self.sent.wait()
         if k == 0:
             return self.first[0] + self.first[1]
         t = self.rest
@@ -329,36 +342,33 @@
 ROWS = 384
 
 
-def fused_kernel(slots_ref, owner_ref, tok_ref, gain_ref, bias_ref, kw_ref, cot_ref,
+def fused_kernel(slots_ref, tok_ref, gain_ref, bias_ref, kw_ref, cot_ref,
                  proj, grad_out, slab_out, gain_out, bias_out,
                  w, kws, held, g, half, slot, seen, fin, first, rest,
-                 tok, normed, cot, inv, coef, small_v, even, odd, send, recv, local, *flat):
+                 tok, normed, cot, inv, coef, small_v, even, odd, owner, send, recv, local, *flat):
     place = Place()
-    wires = Wires(send, recv, 220)
+    wires = Wires(send, recv, SEMS)
     grad_scale = float(ROWS * 128) ** (-0.5)
-    loads = []
-
-    def load(src, dst):
-        copy = pltpu.make_async_copy(src, dst, local.at[len(loads)])
+
+    def load(src, dst, i):
+        copy = pltpu.make_async_copy(src, dst, local.at[i])
         copy.start()
-        loads.append(copy)
         return copy
 
     wait_greet = greet(place)
-    slabs = []
     for i in range(2):
         xh = place.xh if i == 0 else 1 - place.xh
         xl = place.xl if i == 0 else 1 - place.xl
         for t in range(4):
             col = pl.ds(pl.multiple_of((xh * 4 + t) * 128, 128), 128)
-            slabs.append(load(kw_ref.at[:, xl * 4 + place.y, :, col], kws.at[i, t]))
-    rows = [load(tok_ref.at[pl.ds(i * 64, 64)], tok.at[pl.ds(i * 64, 64)]) for i in range(6)]
-    cots = load(cot_ref, cot)
+            load(kw_ref.at[:, xl * 4 + place.y, :, col], kws.at[i, t], 0)
+    rows = [load(tok_ref.at[pl.ds(i * 64, 64)], tok.at[pl.ds(i * 64, 64)], i + 1) for i in range(6)]
+    cots = load(cot_ref, cot, 7)
 
     def norm(i):
         rows[i].wait()
 
-        @pl.loop(i * 4, i * 4 + 4)
+        @pl.loop(i * 4, i * 4 + 4, unroll=2)
         def _(t):
             r = pl.ds(pl.multiple_of(t * 16, 16), 16)
             acc = [jnp.zeros((16, 128), F32)] * 4
@@ -394,10 +404,9 @@
         off, nb = PARTS[p][:2]
         side = own if mine else other
         if mine:
-            swap[p].wait_recv()
-
-        @pl.loop(0, nb // 2)
-        def _(t):
+            swap[p].wait()
+
+        for t in range(nb // 2):
             blocks(side, off + 2 * t, 2, mine)
 
         if nb % 2:
@@ -410,19 +419,17 @@
     gather = Gather(place, wires, w)
     scatter = Scatter(place, wires, g, scatter_bufs(flat))
     small = Small(place, wires, first, rest)
-    come = []
+    come = wires.group(held.at[pl.ds(0, 60)])
 
     def trade_weights():
-        for copy in slabs:
-            copy.wait()
+        pltpu.make_async_copy(kws, kws, local.at[0]).wait()
         mine = held.at[pl.ds(place.big * 4, 4)]
         for i, j, _, device in place.group():
-            come.append(wires.put(kws.at[i, place.at(2, j)], mine, device))
+            come.put(kws.at[i, place.at(2, j)], mine, device)
         held[pl.ds(place.big * 4, 4)] = kws[0, place.z]
 
     def pick():
-        for copy in come:
-            copy.wait_recv()
+        come.wait()
 
         @pl.loop(0, HALF)
         def _(t):
@@ -434,12 +441,11 @@
             small_v[40 + j:41 + j, :] = jnp.sum(
                 cot[:, j * 128:(j + 1) * 128].astype(F32), axis=0, keepdims=True) * grad_scale
 
-    def forward():
-        for copy in gather.pair:
-            copy.wait_recv()
-        coef[...] = jnp.zeros_like(coef)
-
-        @pl.loop(0, 4)
+    def forward(low, high):
+        if low == 0:
+            coef[...] = jnp.zeros_like(coef)
+
+        @pl.loop(low, high)
         def _(n):
             q = 2 * n
             x0, z0 = lax.div(q, 4) * 2, lax.rem(q, 4)
@@ -452,8 +458,9 @@
             both = value * cot[:, col].astype(F32)
             coef[...] += both[:, :128] + both[:, 128:]
 
-        coef[...] = jnp.broadcast_to(
-            jnp.sum(coef[...], axis=1, keepdims=True), (ROWS, 128)) * inv[...] * (1.0 / WIDTH)
+        if high == 4:
+            coef[...] = jnp.broadcast_to(
+                jnp.sum(coef[...], axis=1, keepdims=True), (ROWS, 128)) * inv[...] * (1.0 / WIDTH)
 
     def product(t, into):
         b = 2 * t
@@ -466,27 +473,37 @@
         b = 2 * t
         for i in range(2):
             col = pl.ds(pl.multiple_of((b + i) * 128, 128), 128)
-            gn = grad[:, i * 128:(i + 1) * 128]
-            scale = inv[...]
-            unit = tok[:, col].astype(F32) * scale
-            small_v[pl.ds(b + i, 1), :] = jnp.sum(gn * unit, axis=0, keepdims=True) * grad_scale
-            grad_out[:, col] = (gn * gain_ref[:, col] * scale - unit * coef[...]).astype(BF)
-
-    def backward(low, high):
-        if low == 0:
-            product(0, even)
-
-        @pl.loop(low, min(high, 9))
+            gn = grad[:, i * 128:(i + 1) * 128] * inv[...]
+            small_v[pl.ds(b + i, 1), :] = jnp.sum(gn * tok[:, col].astype(F32), axis=0, keepdims=True) * grad_scale
+            grad_out[:, col] = (gn * gain_ref[:, col]).astype(BF)
+
+    def backward(mine, part):
+        t0 = (place.c if mine else 1 - place.c) * (HALF // 2)
+        if part == 0:
+            if not mine:
+                gather.pair.wait()
+            product(t0, even)
+
+        @pl.loop(2 * part, 2 * part + 2)
         def _(u):
-            product(2 * u + 1, odd)
-            apply(2 * u, even)
-            product(2 * u + 2, even)
-            apply(2 * u + 1, odd)
-
-        if high == 10:
-            product(19, odd)
-            apply(18, even)
-            apply(19, odd)
+            t = t0 + 2 * u
+            product(t + 1, odd)
+            apply(t, even)
+            product(t + 2, even)
+            apply(t + 1, odd)
+
+        if part == 1:
+            product(t0 + 9, odd)
+            apply(t0 + 8, even)
+            apply(t0 + 9, odd)
+
+    def project_out(low, high):
+        @pl.loop(low, high)
+        def _(t):
+            col = pl.ds(pl.multiple_of(t * 256, 256), 256)
+            along = coef[...] * inv[...]
+            along = jnp.concatenate([along, along], axis=1)
+            grad_out[:, col] = (grad_out[:, col].astype(F32) - tok[:, col].astype(F32) * along).astype(BF)
 
     def each(step, k, *part):
         for p in range(3):
@@ -500,69 +517,82 @@
         gain_out[...] = total[:40]
         bias_out[...] = total[40:]
 
-    back = []
+    back = wires.group(slot.at[pl.ds(0, 60)])
+
+    def invert():
+        @pl.loop(0, 64)
+        def _(t):
+            found = jnp.int32(-1)
+            for b in range(40):
+                found = jnp.where(slots_ref[b] == t, b, found)
+            owner[t] = found
 
     def trade_grads():
         @pl.loop(0, 64)
         def _(t):
-            b = owner_ref[t]
+            b = owner[t]
             ours = jnp.logical_and(b >= own, b < own + HALF)
             value = g[place.x, place.y, place.z, jnp.maximum(b, 0)]
             slot[t] = jnp.where(ours, value, jnp.zeros_like(value))
 
         for _, _, _, device in place.group():
-            back.append(wires.put(
-                slot.at[pl.ds(device[0] * 4, 4)], seen.at[place.c, place.xh, place.z], device))
+            back.put(slot.at[pl.ds(device[0] * 4, 4)], seen.at[place.c, place.xh, place.z], device)
         seen[place.c, place.xh, place.z] = slot[pl.ds(place.big * 4, 4)]
 
     pi, y = place.pi, place.y
     yup, ydown = place.ring(1, 1), place.ring(1, 3)
     below, above, across = place.at(1, 3), place.at(1, 1), place.at(1, 2)
     sent = {}
+    last = wires.group(fin.at[0])
 
     def move(name, side, row, slot0, count, device):
         ref = fin.at[side, row, pl.ds(slot0, count)]
-        sent[name] = wires.put(ref, ref, device)
-
-    def ring(name, side, slot0):
-        move(name + "u0", side, y, slot0, 1, yup)
-        move(name + "d1", side, y, slot0 + 1, 1, ydown)
-        move(name + "u1", side, y, slot0 + 1, 1, yup)
-        move(name + "d0", side, y, slot0, 1, ydown)
-
-    def ring_on(name, side, slot0):
-        sent[name + "u0"].wait_recv()
-        move(name + "f0", side, below, slot0, 1, yup)
-        sent[name + "d1"].wait_recv()
-        move(name + "f1", side, above, slot0 + 1, 1, ydown)
+        if name in sent:
+            sent[name].put(ref, ref, device)
+        elif name:
+            sent[name] = wires.put(ref, ref, device)
+        else:
+            last.put(ref, ref, device)
+
+    def ring(name, side, slot0, late):
+        move(name + "u", side, y, slot0, 1, yup)
+        move(name + "d", side, y, slot0 + 1, 1, ydown)
+        move(late, side, y, slot0 + 1, 1, yup)
+        move(late, side, y, slot0, 1, ydown)
+
+    def ring_on(name, side, slot0, late):
+        sent[name + "u"].wait()
+        move(late, side, below, slot0, 1, yup)
+        sent[name + "d"].wait()
+        move(late, side, above, slot0 + 1, 1, ydown)
 
     def spread_start():
-        for copy in back:
-            copy.wait_recv()
+        back.wait()
         for q in range(8):
             fin[pi, y, :, q // 4, q % 4] = seen[0, q // 4, q % 4] + seen[1, q // 4, q % 4]
+        sent["c1"] = wires.group(fin.at[0, 0, pl.ds(0, 2)])
+        sent["c2"] = wires.group(fin.at[0, 0, pl.ds(0, 2)])
         move("px", pi, y, 0, 2, place.x_pair())
-        ring("a", pi, 0)
-        move("qx", pi, y, 2, 2, place.x_pair())
-        ring("c", pi, 2)
+        ring("a", pi, 0, "")
+        move("", pi, y, 2, 2, place.x_pair())
+        ring("c", pi, 2, "c1")
 
     def spread_middle():
-        sent["px"].wait_recv()
-        ring("b", 1 - pi, 0)
-        ring_on("a", pi, 0)
-        ring_on("c", pi, 2)
-        sent["cu1"].wait_recv()
-        move("rx", pi, below, 2, 2, place.x_pair())
-        sent["cd0"].wait_recv()
-        move("sx", pi, above, 2, 2, place.x_pair())
+        sent["px"].wait()
+        ring("b", 1 - pi, 0, "")
+        ring_on("a", pi, 0, "")
+        ring_on("c", pi, 2, "c2")
+        sent["c1"].wait()
+        move("", pi, below, 2, 2, place.x_pair())
+        move("", pi, above, 2, 2, place.x_pair())
+
+    def spread_late():
+        ring_on("b", 1 - pi, 0, "")
+        sent["c2"].wait()
+        move("", pi, across, 2, 2, place.x_pair())
 
     def spread_end():
-        sent["cf0"].wait_recv()
-        sent["cf1"].wait_recv()
-        move("tx", pi, across, 2, 2, place.x_pair())
-        ring_on("b", 1 - pi, 0)
-        for name in ("au1", "ad0", "af0", "af1", "bu1", "bd0", "bf0", "bf1", "qx", "rx", "sx", "tx"):
-            sent[name].wait_recv()
+        last.wait()
 
         @pl.loop(0, 32)
         def _(t):
@@ -571,10 +601,9 @@
                 side = lax.rem(lax.div(r, 4) + q // 4, 2)
                 slab_out[i, r, :, q * 128:(q + 1) * 128] = fin[side, lax.rem(r, 4), i, q // 4, q % 4].astype(F32)
 
-    for i in range(3): norm(i)
     wait_greet()
     trade_weights()
-    for i in range(3, 6): norm(i)
+    for i in range(6): norm(i)
     cots.wait()
     partial(0, False)
     partial(1, False)
@@ -584,36 +613,46 @@
     partial(0, True)
     each(gather.finish, 0)
     each(gather.start, 1)
+    scatter.start(0, 0, 0)
     partial(1, True)
+    scatter.start(1, 0, 0)
     partial(2, True)
+    scatter.start(2, 0, 0)
     each(gather.forward, 1)
-    each(scatter.start, 0, 0)
+    each(scatter.start, 0, 1)
     bias_sum()
+    invert()
+    each(scatter.forward, 0)
     each(gather.finish, 1)
-    each(gather.start, 2)
-    each(scatter.start, 0, 1)
-    each(gather.forward, 2)
-    each(scatter.forward, 0)
-    each(gather.finish, 2)
-    forward()
+    each(gather.start, 2, 0)
     each(scatter.finish, 0)
     each(scatter.start, 1)
-    backward(0, 4)
+    each(gather.start, 2, 1)
     each(scatter.forward, 1)
-    backward(4, 8)
+    each(gather.forward, 2)
     each(scatter.finish, 1)
     each(scatter.start, 2)
-    backward(8, 10)
+    each(gather.arrive, 2)
+    each(gather.finish, 2)
+    backward(True, 0)
+    each(scatter.finish, 2)
+    trade_grads()
+    backward(True, 1)
+    backward(False, 0)
+    spread_start()
+    backward(False, 1)
     small.start(0, small_v[...])
     small_next(0)
-    each(scatter.finish, 2)
-    trade_grads()
+    spread_middle()
+    forward(0, 1)
     small_next(1)
-    spread_start()
+    forward(1, 3)
+    spread_late()
     small_next(2)
-    spread_middle()
+    forward(3, 4)
+    project_out(0, 20)
+    spread_end()
     small_end()
-    spread_end()
     wires.drain()
 
 
@@ -632,6 +671,7 @@
 LIMIT = 56 * 1024 * 1024
 
 
+SEMS = 65
 OUTS = (
     ((ROWS, KEYS), BF),
     ((ROWS, WIDTH), BF),
@@ -641,11 +681,11 @@
 )
 
 
-def fused(block_slot, owner, tokens, gain, bias, key_weight, cotangent):
+def fused(block_slot, tokens, gain, bias, key_weight, cotangent):
     outs = pl.pallas_call(
         fused_kernel,
         out_shape=tuple(pltpu.VMEM(*out) for out in OUTS),
-        in_specs=[SM, SM, ANY, VM, VM, ANY, ANY],
+        in_specs=[SM, ANY, VM, VM, ANY, ANY],
         out_specs=(VM,) * 5,
         scratch_shapes=[
             pltpu.VMEM((4, 4, 4, 40, 16, 128), BF),
@@ -666,13 +706,14 @@
             pltpu.VMEM((48, 128), F32),
             pltpu.VMEM((ROWS, 256), F32),
             pltpu.VMEM((ROWS, 256), F32),
-            pltpu.SemaphoreType.DMA((220,)),
-            pltpu.SemaphoreType.DMA((220,)),
-            pltpu.SemaphoreType.DMA((40,)),
+            pltpu.SMEM((64,), jnp.int32),
+            pltpu.SemaphoreType.DMA((SEMS,)),
+            pltpu.SemaphoreType.DMA((SEMS,)),
+            pltpu.SemaphoreType.DMA((8,)),
         ] + scatter_scratch(),
         compiler_params=pltpu.CompilerParams(collective_id=0, has_side_effects=True, vmem_limit_bytes=LIMIT),
         name="fused",
-    )(block_slot, owner, tokens, gain, bias, key_weight, cotangent)
+    )(block_slot, tokens, gain, bias, key_weight, cotangent)
     return pl.pallas_call(
         emit_kernel,
         out_shape=tuple(jax.ShapeDtypeStruct(*out) for out in OUTS),
@@ -685,11 +726,8 @@
 
 
 def local(tokens, norm_gain, key_bias, key_weight, cotangent, block_slot):
-    slots = jnp.arange(64, dtype=jnp.int32)
-    hit = block_slot[None, :] == slots[:, None]
-    owner = jnp.max(jnp.where(hit, jnp.arange(40, dtype=jnp.int32)[None, :], -1), axis=1)
     projected, token_grad, slab, gain, bias = fused(
-        block_slot, owner, tokens, norm_gain.reshape(1, WIDTH), key_bias.reshape(1, KEYS),
+        block_slot, tokens, norm_gain.reshape(1, WIDTH), key_bias.reshape(1, KEYS),
         key_weight.reshape(4, 8, 16, KEYS), cotangent)
     return (projected, token_grad, slab.reshape(512, KEYS), gain.reshape(-1), bias.reshape(-1))
 

time: 100 us -> 84.5 us (0.84)
  Pallas kernels: 98.4 us -> 83.7 us
  other arithmetic: 1.26 us -> 0 us
    pallas_call x1, Pallas kernels: 95.4 us -> 80.8 us  [fused(): pl.pallas_call(fused_kernel, out_shape=tuple((pltpu.VMEM(*out) for out in...]
    reduce_max x1 -> x0, other arithmetic: 1.26 us -> none  [local(): jnp.max(jnp.where(hit, jnp.arange(40, dtype=jnp.int32)[None, :], -1), axi...]
where the time goes in v4:
time: 84.5 us; the launch traced here: 84.4 us
  Pallas kernels  83.7 us (99%)
    pallas_call x1, Pallas kernels, fused(): pl.pallas_call(fused_kernel, out_shape=tuple((pltpu.VMEM(*out) for out in...  80.8 us
    pallas_call x1, Pallas kernels, fused(): pl.pallas_call(emit_kernel, out_shape=tuple((jax.ShapeDtypeStruct(*out) f...  2.92 us

profile of v4, /device:TPU:0, one launch (start us, length us, event | category | flops | bytes accessed | tf_op | source)
XLA Modules:
  0.0 84.4 jit_solution(486762685459373608)
XLA Ops:
  0.6 80.8 %fused.1 = (bf16[384,1024]{1,0:T(8,128)(2,1)S(1)}, bf16[384,5120]{1,0:T(8,128)(2,1)S(1)}, f32[4,8,16,1024]{3,2,1,0:T(8,128)S(1)}, f32[40,128]{1,0:T(8,128)S(1)}, f32[8,128]{1,0:T(8,128)S(1)}) custom-call(s32[40]{0:T(128)} %slots_ref.1, bf16[384,5120]{1,0:T(8,128)(2,1)} %tok_ref.1, f32[1,5120]{1,0:T(1,128)} %bitcast.7, f32[1,1024]{1,0:T(1,128)} %bitcast.8, ...), custom_call_target="tpu_custom_call" | custom-call | tf_op jit(solution)/shard_map/fused/pallas_call | solution.py:685
  81.4 2.9 %emit.1 = (bf16[384,1024]{1,0:T(8,128)(2,1)}, bf16[384,5120]{1,0:T(8,128)(2,1)}, f32[4,8,16,1024]{3,2,1,0:T(8,128)}, f32[40,128]{1,0:T(8,128)}, f32[8,128]{1,0:T(8,128)}) custom-call(bf16[384,1024]{1,0:T(8,128)(2,1)S(1)} %get-tuple-element.15.refs_0_, bf16[384,5120]{1,0:T(8,128)(2,1)S(1)} %get-tuple-element.16.refs_1_, ...), custom_call_target="tpu_custom_call" | custom-call | tf_op jit(solution)/shard_map/emit/pallas_call | solution.py:717

commit v5 on v4

--- a/solution.py
+++ b/solution.py
@@ -118,12 +118,20 @@
     return tuple(out)
 
 
+BATCHES = (
+    ((0, 4, 2), (4, 3, 2)),
+    ((0, 4, 2), (4, 3, 1)),
+    ((0, 2, 1), (2, 4, 2)),
+)
+
+
 class Gather:
     def __init__(self, place, wires, w):
         self.place, self.wires, self.w = place, wires, w
         self.base = place.c * HALF
         self.stage = {}
-        self.pair = wires.group(w.at[:, :, :, pl.ds(0, HALF)])
+        half = HALF // 2
+        self.pair = [wires.group(w.at[:, :, :, pl.ds(0, half)]) for _ in range(2)]
 
     def view(self, p, k, v, first, count):
         off, nb, h, order = PARTS[p]
@@ -133,67 +141,73 @@
 
     def move(self, group, p, k, v, first, count, device):
         ref = self.view(p, k, v, first, count)
-        (group or self.wires.group(ref)).put(ref, ref, device)
-        return group or self.wires.groups[-1]
-
-    def start(self, p, k, part=None):
-        off, nb, h, order = PARTS[p]
-        place, axis, group = self.place, order[k], self.wires.group
+        group = group or self.wires.group(ref)
+        group.put(ref, ref, device)
+        return group
+
+    def span(self, p, k, batch):
+        first, n, h = (0,) + PARTS[p][1:3] if k < 2 else BATCHES[p][batch]
+        return first, h, n - h
+
+    def start(self, p, k, batch=0, part=None):
+        place, axis, group = self.place, PARTS[p][3][k], self.wires.group
+        first, lo, hi = self.span(p, k, batch)
+        mid = first + lo
         me = place.pos[axis]
         up, down = place.ring(axis, 1), place.ring(axis, 3)
         if k == 0:
-            both = group(self.w.at[0, 0, 0, pl.ds(0, 3 * nb)])
+            both = group(self.w.at[0, 0, 0, pl.ds(0, 3 * (lo + hi))])
             for device in (place.ring(axis, 2), up, down):
-                self.move(both, p, k, me, 0, nb, device)
-            self.stage[p, k] = both
+                self.move(both, p, k, me, 0, lo + hi, device)
+            self.stage[p, k, 0] = both
             return
         if part != 1:
-            u0 = self.move(None, p, k, me, 0, h, up)
-            d1 = self.move(None, p, k, me, h, nb - h, down)
-            self.stage[p, k] = [u0, d1]
+            u0 = self.move(None, p, k, me, first, lo, up)
+            d1 = self.move(None, p, k, me, mid, hi, down)
+            self.stage[p, k, batch] = [u0, d1]
         if part != 0:
-            one = self.w.at[0, :, :, pl.ds(0, nb)]
-            two = self.w.at[0, pl.ds(0, 2), :, pl.ds(0, nb)]
+            one = self.w.at[0, :, :, pl.ds(0, lo + hi)]
+            two = self.w.at[0, pl.ds(0, 2), :, pl.ds(0, lo + hi)]
             late = group(one if k == 2 else two)
-            self.move(late, p, k, me, h, nb - h, up)
-            self.move(late, p, k, me, 0, h, down)
-            self.stage[p, k] += [late, group(one) if k == 2 else late]
-
-    def share(self, p, k, v, first, count):
+            self.move(late, p, k, me, mid, hi, up)
+            self.move(late, p, k, me, first, lo, down)
+            self.stage[p, k, batch] += [late, group(one) if k == 2 else late]
+
+    def share(self, p, k, v, first, count, batch):
         if k == 2:
-            self.move(self.pair, p, k, v, first, count, self.place.partner())
-
-    def forward(self, p, k):
-        off, nb, h, order = PARTS[p]
-        place, axis = self.place, order[k]
-        u0, d1, late, last = self.stage[p, k]
+            self.move(self.pair[batch], p, k, v, first, count, self.place.partner())
+
+    def forward(self, p, k, batch=0):
+        place, axis = self.place, PARTS[p][3][k]
+        first, lo, hi = self.span(p, k, batch)
+        u0, d1, late, last = self.stage[p, k, batch]
         below, above = place.at(axis, 3), place.at(axis, 1)
         u0.wait()
-        self.move(last, p, k, below, 0, h, place.ring(axis, 1))
+        self.move(last, p, k, below, first, lo, place.ring(axis, 1))
         d1.wait()
-        self.move(last, p, k, above, h, nb - h, place.ring(axis, 3))
-        self.share(p, k, below, 0, h)
-        self.share(p, k, above, h, nb - h)
-
-    def arrive(self, p, k):
-        off, nb, h, order = PARTS[p]
+        self.move(last, p, k, above, first + lo, hi, place.ring(axis, 3))
+        self.share(p, k, below, first, lo, batch)
+        self.share(p, k, above, first + lo, hi, batch)
+
+    def arrive(self, p, k, batch=0):
+        place, axis = self.place, PARTS[p][3][k]
+        first, lo, hi = self.span(p, k, batch)
+        self.stage[p, k, batch][2].wait()
+        self.share(p, k, place.at(axis, 3), first + lo, hi, batch)
+        self.share(p, k, place.at(axis, 1), first, lo, batch)
+
+    def finish(self, p, k, batch=0):
+        order = PARTS[p][3]
         place, axis = self.place, order[k]
-        self.stage[p, k][2].wait()
-        self.share(p, k, place.at(axis, 3), h, nb - h)
-        self.share(p, k, place.at(axis, 1), 0, h)
-
-    def finish(self, p, k):
-        off, nb, h, order = PARTS[p]
-        place, axis = self.place, order[k]
+        first, lo, hi = self.span(p, k, batch)
         if k == 0:
-            self.stage[p, k].wait()
+            self.stage[p, k, 0].wait()
             return
-        self.stage[p, k][3].wait()
-        across = place.at(axis, 2)
-        self.share(p, k, across, 0, h)
-        self.share(p, k, across, h, nb - h)
+        self.stage[p, k, batch][3].wait()
+        self.share(p, k, place.at(axis, 2), first, lo + hi, batch)
         if k == 1:
-            self.share(p, 2, place.pos[order[2]], 0, nb)
+            for i, (start, n, _) in enumerate(BATCHES[p]):
+                self.share(p, 2, place.pos[order[2]], start, n, i)
 
 
 def rest_of(t, count):
@@ -322,9 +336,9 @@
             own = self.first.at[place.c]
             self.sent = self.wires.put(own, own, place.partner())
             return
-        axis = k - 1
-        self.rest[axis, place.pos[axis]] = value
-        own = self.rest.at[axis, place.pos[axis]]
+        axis = 3 - k
+        self.rest[k - 1, place.pos[axis]] = value
+        own = self.rest.at[k - 1, place.pos[axis]]
         self.sent = self.wires.group(self.rest.at[0, pl.ds(0, 3)])
         for step in (2, 1, 3):
             self.sent.put(own, own, place.ring(axis, step))
@@ -342,10 +356,10 @@
 ROWS = 384
 
 
-def fused_kernel(slots_ref, tok_ref, gain_ref, bias_ref, kw_ref, cot_ref,
+def fused_kernel(slots_hbm, tok_ref, gain_hbm, bias_hbm, kw_ref, cot_ref,
                  proj, grad_out, slab_out, gain_out, bias_out,
                  w, kws, held, g, half, slot, seen, fin, first, rest,
-                 tok, normed, cot, inv, coef, small_v, even, odd, owner, send, recv, local, *flat):
+                 tok, normed, cot, inv, coef, small_v, even, odd, keys, owner, slots_ref, gain_ref, bias_ref, send, recv, local, *flat):
     place = Place()
     wires = Wires(send, recv, SEMS)
     grad_scale = float(ROWS * 128) ** (-0.5)
@@ -355,6 +369,7 @@
         copy.start()
         return copy
 
+    gains = load(gain_hbm, gain_ref, 8)
     wait_greet = greet(place)
     for i in range(2):
         xh = place.xh if i == 0 else 1 - place.xh
@@ -364,9 +379,13 @@
             load(kw_ref.at[:, xl * 4 + place.y, :, col], kws.at[i, t], 0)
     rows = [load(tok_ref.at[pl.ds(i * 64, 64)], tok.at[pl.ds(i * 64, 64)], i + 1) for i in range(6)]
     cots = load(cot_ref, cot, 7)
+    slot_list = load(slots_hbm, slots_ref, 9)
+    biases = load(bias_hbm, bias_ref, 10)
 
     def norm(i):
         rows[i].wait()
+        if i == 0:
+            gains.wait()
 
         @pl.loop(i * 4, i * 4 + 4, unroll=2)
         def _(t):
@@ -386,36 +405,66 @@
     other = (1 - place.c) * HALF
     full = (slice(None),) * 3
 
-    def blocks(side, first, count, add):
+    def blocks(side, first, count):
         b = side + first
         left = normed[:, pl.ds(pl.multiple_of(b * 128, 128), count * 128)]
         value = lax.dot_general(left, cot[...], (((0,), (0,)), ((), ())), preferred_element_type=F32)
-        value = value * grad_scale
+        value = (value * grad_scale).astype(BF)
         for i in range(count):
             for r in range(8):
                 for q in range(8):
-                    at = (q // 4 * 2 + r // 4, r % 4, q % 4)
-                    tile = value[i * 128 + r * 16:i * 128 + r * 16 + 16, q * 128:(q + 1) * 128]
-                    if add:
-                        tile = tile + half[at + (first + i,)].astype(F32)
-                    g[at + (b + i,)] = tile.astype(BF)
+                    g[q // 4 * 2 + r // 4, r % 4, q % 4, b + i] = value[
+                        i * 128 + r * 16:i * 128 + r * 16 + 16, q * 128:(q + 1) * 128]
 
     def partial(p, mine):
         off, nb = PARTS[p][:2]
         side = own if mine else other
-        if mine:
-            swap[p].wait()
-
         for t in range(nb // 2):
-            blocks(side, off + 2 * t, 2, mine)
-
+            blocks(side, off + 2 * t, 2)
         if nb % 2:
-            blocks(side, off + nb - 1, 1, mine)
-        if not mine:
-            swap.append(wires.put(
-                g.at[full + (pl.ds(other + off, nb),)], half.at[full + (pl.ds(off, nb),)], place.partner()))
-
-    swap = []
+            blocks(side, off + nb - 1, 1)
+
+    def plane(p, step):
+        axis = PARTS[p][3][0]
+        at = [slice(None)] * 3
+        at[axis] = place.at(axis, step)
+        return axis, tuple(at)
+
+    def swap(p, step, group=None):
+        off, nb = PARTS[p][:2]
+        _, at = plane(p, step)
+        dst = half.at[at + (pl.ds(off, nb),)]
+        group = group or wires.group(dst)
+        group.put(g.at[at + (pl.ds(other + off, nb),)], dst, place.partner())
+        return group
+
+    def swap_rest(p):
+        group = wires.group(half.at[pl.ds(0, 3), :, :, pl.ds(0, PARTS[p][1])])
+        for step in (1, 3, 0):
+            swap(p, step, group)
+        return group
+
+    def merge(p, *steps):
+        off, nb = PARTS[p][:2]
+        for step in steps:
+            axis, at = plane(p, step)
+
+            @pl.loop(0, 16, unroll=2)
+            def _(t):
+                rest = [lax.div(t, 4), lax.rem(t, 4)]
+                rest.insert(axis, at[axis])
+                here = tuple(rest) + (pl.ds(own + off, nb),)
+                g[here] = g[here] + half[tuple(rest) + (pl.ds(off, nb),)]
+
+    def merge_far(p):
+        far[p].wait()
+        merge(p, 2)
+
+    def merge_near(p):
+        near[p].wait()
+        merge(p, 1, 3, 0)
+
+    far, near = [], []
     gather = Gather(place, wires, w)
     scatter = Scatter(place, wires, g, scatter_bufs(flat))
     small = Small(place, wires, first, rest)
@@ -430,6 +479,7 @@
 
     def pick():
         come.wait()
+        slot_list.wait()
 
         @pl.loop(0, HALF)
         def _(t):
@@ -437,72 +487,83 @@
             w[place.x, place.y, place.z, b] = held[slots_ref[b]]
 
     def bias_sum():
+        biases.wait()
         for j in range(8):
             small_v[40 + j:41 + j, :] = jnp.sum(
                 cot[:, j * 128:(j + 1) * 128].astype(F32), axis=0, keepdims=True) * grad_scale
 
-    def forward(low, high):
-        if low == 0:
-            coef[...] = jnp.zeros_like(coef)
+    def early(batch):
+        return [PARTS[p][0] + BATCHES[p][batch][0] + i for p in range(3) for i in range(BATCHES[p][batch][1])]
+
+    def forward(batch, low, high):
+        some = [side * HALF + b for side in range(2) for b in early(batch)]
 
         @pl.loop(low, high)
         def _(n):
             q = 2 * n
             x0, z0 = lax.div(q, 4) * 2, lax.rem(q, 4)
+            left = jnp.concatenate([normed[:, b * 128:(b + 1) * 128] for b in some], axis=1)
             right = jnp.concatenate(
                 [jnp.concatenate([w[x0 + r // 4, r % 4, z0, b], w[x0 + r // 4, r % 4, z0 + 1, b]], axis=1)
-                 for b in range(40) for r in range(8)], axis=0)
-            value = jnp.dot(normed[...], right, preferred_element_type=F32)
+                 for b in some for r in range(8)], axis=0)
+            value = jnp.dot(left, right, preferred_element_type=F32)
             col = pl.ds(pl.multiple_of(n * 256, 256), 256)
+            if batch == 0:
+                keys[:, col] = value
+                return
+            value = value + keys[:, col]
             proj[:, col] = (value + bias_ref[:, col]).astype(BF)
             both = value * cot[:, col].astype(F32)
-            coef[...] += both[:, :128] + both[:, 128:]
-
-        if high == 4:
+            both = both[:, :128] + both[:, 128:]
+            if low == 0:
+                both = jnp.where(n == 0, 0.0, coef[...]) + both
+            else:
+                both = coef[...] + both
+            coef[...] = both
+
+        if batch == 1 and high == 4:
             coef[...] = jnp.broadcast_to(
-                jnp.sum(coef[...], axis=1, keepdims=True), (ROWS, 128)) * inv[...] * (1.0 / WIDTH)
-
-    def product(t, into):
-        b = 2 * t
+                jnp.sum(coef[...], axis=1, keepdims=True), (ROWS, 128)) * inv[...] * inv[...] * (1.0 / WIDTH)
+
+    def product(side, pair, into):
         right = jnp.concatenate(
-            [jnp.concatenate([w[q // 4 * 2 + r // 4, r % 4, q % 4, b + i] for q in range(8)], axis=1)
-             for i in range(2) for r in range(8)], axis=0)
+            [jnp.concatenate([w[q // 4 * 2 + r // 4, r % 4, q % 4, side + b] for q in range(8)], axis=1)
+             for b in pair for r in range(8)], axis=0)
         into[...] = lax.dot_general(cot[...], right, (((1,), (1,)), ((), ())), preferred_element_type=F32)
 
-    def apply(t, grad):
-        b = 2 * t
-        for i in range(2):
-            col = pl.ds(pl.multiple_of((b + i) * 128, 128), 128)
+    def apply(side, pair, grad):
+        for i, b in enumerate(pair):
+            col = pl.ds(pl.multiple_of((side + b) * 128, 128), 128)
             gn = grad[:, i * 128:(i + 1) * 128] * inv[...]
-            small_v[pl.ds(b + i, 1), :] = jnp.sum(gn * tok[:, col].astype(F32), axis=0, keepdims=True) * grad_scale
+            small_v[pl.ds(side + b, 1), :] = jnp.sum(
+                gn * tok[:, col].astype(F32), axis=0, keepdims=True) * grad_scale
             grad_out[:, col] = (gn * gain_ref[:, col]).astype(BF)
 
-    def backward(mine, part):
-        t0 = (place.c if mine else 1 - place.c) * (HALF // 2)
-        if part == 0:
-            if not mine:
-                gather.pair.wait()
-            product(t0, even)
-
-        @pl.loop(2 * part, 2 * part + 2)
-        def _(u):
-            t = t0 + 2 * u
-            product(t + 1, odd)
-            apply(t, even)
-            product(t + 2, even)
-            apply(t + 1, odd)
-
-        if part == 1:
-            product(t0 + 9, odd)
-            apply(t0 + 8, even)
-            apply(t0 + 9, odd)
+    def backward(batch, side):
+        some = early(batch)
+        pairs = [some[i:i + 2] for i in range(0, len(some), 2)]
+        product(side, pairs[0], even)
+        for i, pair in enumerate(pairs):
+            here, there = (even, odd) if i % 2 == 0 else (odd, even)
+            if i + 1 < len(pairs):
+                product(side, pairs[i + 1], there)
+            apply(side, pair, here)
+
+    def backward_early(mine):
+        if not mine:
+            gather.pair[0].wait()
+        backward(0, own if mine else other)
+
+    def backward_late(mine):
+        if not mine:
+            gather.pair[1].wait()
+        backward(1, own if mine else other)
 
     def project_out(low, high):
         @pl.loop(low, high)
         def _(t):
             col = pl.ds(pl.multiple_of(t * 256, 256), 256)
-            along = coef[...] * inv[...]
-            along = jnp.concatenate([along, along], axis=1)
+            along = jnp.concatenate([coef[...], coef[...]], axis=1)
             grad_out[:, col] = (grad_out[:, col].astype(F32) - tok[:, col].astype(F32) * along).astype(BF)
 
     def each(step, k, *part):
@@ -528,7 +589,7 @@
             owner[t] = found
 
     def trade_grads():
-        @pl.loop(0, 64)
+        @pl.loop(0, 64, unroll=4)
         def _(t):
             b = owner[t]
             ours = jnp.logical_and(b >= own, b < own + HALF)
@@ -573,23 +634,25 @@
         sent["c1"] = wires.group(fin.at[0, 0, pl.ds(0, 2)])
         sent["c2"] = wires.group(fin.at[0, 0, pl.ds(0, 2)])
         move("px", pi, y, 0, 2, place.x_pair())
+        ring("c", pi, 2, "c1")
         ring("a", pi, 0, "")
         move("", pi, y, 2, 2, place.x_pair())
-        ring("c", pi, 2, "c1")
+
+    def spread_on():
+        ring_on("c", pi, 2, "c2")
 
     def spread_middle():
         sent["px"].wait()
         ring("b", 1 - pi, 0, "")
-        ring_on("a", pi, 0, "")
-        ring_on("c", pi, 2, "c2")
         sent["c1"].wait()
         move("", pi, below, 2, 2, place.x_pair())
         move("", pi, above, 2, 2, place.x_pair())
+        ring_on("a", pi, 0, "")
 
     def spread_late():
-        ring_on("b", 1 - pi, 0, "")
         sent["c2"].wait()
         move("", pi, across, 2, 2, place.x_pair())
+        ring_on("b", 1 - pi, 0, "")
 
     def spread_end():
         last.wait()
@@ -601,55 +664,73 @@
                 side = lax.rem(lax.div(r, 4) + q // 4, 2)
                 slab_out[i, r, :, q * 128:(q + 1) * 128] = fin[side, lax.rem(r, 4), i, q // 4, q % 4].astype(F32)
 
+    for i in range(3): norm(i)
     wait_greet()
     trade_weights()
-    for i in range(6): norm(i)
+    for i in range(3, 6): norm(i)
     cots.wait()
     partial(0, False)
+    far.append(swap(0, 2))
     partial(1, False)
+    far.append(swap(1, 2))
+    partial(2, False)
+    far.append(swap(2, 2))
+    near.extend(swap_rest(p) for p in range(3))
+    partial(0, True)
     pick()
     each(gather.start, 0)
-    partial(2, False)
-    partial(0, True)
+    merge_far(0)
+    scatter.start(0, 0, 0)
+    partial(1, True)
+    merge_far(1)
+    scatter.start(1, 0, 0)
+    partial(2, True)
     each(gather.finish, 0)
     each(gather.start, 1)
-    scatter.start(0, 0, 0)
-    partial(1, True)
-    scatter.start(1, 0, 0)
-    partial(2, True)
+    merge_far(2)
     scatter.start(2, 0, 0)
-    each(gather.forward, 1)
-    each(scatter.start, 0, 1)
+    for p in range(3): merge_near(p); scatter.start(p, 0, 1)
+    for p in (1, 2): gather.forward(p, 1)
+    scatter.forward(0, 0)
+    gather.forward(0, 1)
+    scatter.forward(1, 0)
     bias_sum()
     invert()
-    each(scatter.forward, 0)
-    each(gather.finish, 1)
-    each(gather.start, 2, 0)
-    each(scatter.finish, 0)
-    each(scatter.start, 1)
-    each(gather.start, 2, 1)
+    scatter.forward(2, 0)
+    for p in (2, 0, 1): gather.finish(p, 1); gather.start(p, 2, 0, 0)
+    for p in range(3): scatter.finish(p, 0); scatter.start(p, 1)
+    each(gather.start, 2, 0, 1)
     each(scatter.forward, 1)
-    each(gather.forward, 2)
+    each(gather.forward, 2, 0)
+    each(gather.start, 2, 1, 0)
     each(scatter.finish, 1)
     each(scatter.start, 2)
-    each(gather.arrive, 2)
-    each(gather.finish, 2)
-    backward(True, 0)
+    each(gather.start, 2, 1, 1)
+    each(gather.arrive, 2, 0)
+    each(gather.finish, 2, 0)
+    backward_early(True)
+    each(gather.forward, 2, 1)
     each(scatter.finish, 2)
     trade_grads()
-    backward(True, 1)
-    backward(False, 0)
+    each(gather.arrive, 2, 1)
+    backward_early(False)
+    each(gather.finish, 2, 1)
+    backward_late(True)
     spread_start()
-    backward(False, 1)
+    backward_late(False)
     small.start(0, small_v[...])
+    forward(0, 0, 2)
     small_next(0)
+    spread_on()
+    forward(0, 2, 3)
     spread_middle()
-    forward(0, 1)
+    forward(0, 3, 4)
+    forward(1, 0, 1)
     small_next(1)
-    forward(1, 3)
+    forward(1, 1, 2)
     spread_late()
+    forward(1, 2, 4)
     small_next(2)
-    forward(3, 4)
     project_out(0, 20)
     spread_end()
     small_end()
@@ -671,7 +752,7 @@
 LIMIT = 56 * 1024 * 1024
 
 
-SEMS = 65
+SEMS = 81
 OUTS = (
     ((ROWS, KEYS), BF),
     ((ROWS, WIDTH), BF),
@@ -685,7 +766,7 @@
     outs = pl.pallas_call(
         fused_kernel,
         out_shape=tuple(pltpu.VMEM(*out) for out in OUTS),
-        in_specs=[SM, ANY, VM, VM, ANY, ANY],
+        in_specs=[ANY] * 6,
         out_specs=(VM,) * 5,
         scratch_shapes=[
             pltpu.VMEM((4, 4, 4, 40, 16, 128), BF),
@@ -706,10 +787,14 @@
             pltpu.VMEM((48, 128), F32),
             pltpu.VMEM((ROWS, 256), F32),
             pltpu.VMEM((ROWS, 256), F32),
+            pltpu.VMEM((ROWS, KEYS), F32),
             pltpu.SMEM((64,), jnp.int32),
+            pltpu.SMEM((40,), jnp.int32),
+            pltpu.VMEM((1, WIDTH), F32),
+            pltpu.VMEM((1, KEYS), F32),
             pltpu.SemaphoreType.DMA((SEMS,)),
             pltpu.SemaphoreType.DMA((SEMS,)),
-            pltpu.SemaphoreType.DMA((8,)),
+            pltpu.SemaphoreType.DMA((11,)),
         ] + scatter_scratch(),
         compiler_params=pltpu.CompilerParams(collective_id=0, has_side_effects=True, vmem_limit_bytes=LIMIT),
         name="fused",

time: 84.5 us -> 80 us (0.947)
  Pallas kernels: 83.7 us -> 79.1 us
    pallas_call x1, Pallas kernels: 80.8 us -> 76.2 us  [fused(): pl.pallas_call(fused_kernel, out_shape=tuple((pltpu.VMEM(*out) for out in...]
where the time goes in v5:
time: 80 us; the launch traced here: 79.9 us
  Pallas kernels  79.1 us (99%)
  between operations  0.8 us (1%)
    pallas_call x1, Pallas kernels, fused(): pl.pallas_call(fused_kernel, out_shape=tuple((pltpu.VMEM(*out) for out in...  76.2 us
    pallas_call x1, Pallas kernels, fused(): pl.pallas_call(emit_kernel, out_shape=tuple((jax.ShapeDtypeStruct(*out) f...  2.92 us

profile of v5, /device:TPU:0, one launch (start us, length us, event | category | flops | bytes accessed | tf_op | source)
XLA Modules:
  0.0 79.9 jit_solution(10533689427618116915)
XLA Ops:
  0.6 76.2 %fused.1 = (bf16[384,1024]{1,0:T(8,128)(2,1)S(1)}, bf16[384,5120]{1,0:T(8,128)(2,1)S(1)}, f32[4,8,16,1024]{3,2,1,0:T(8,128)S(1)}, f32[40,128]{1,0:T(8,128)S(1)}, f32[8,128]{1,0:T(8,128)S(1)}) custom-call(s32[40]{0:T(128)} %slots_hbm.1, bf16[384,5120]{1,0:T(8,128)(2,1)} %tok_ref.1, f32[1,5120]{1,0:T(1,128)} %bitcast.7, f32[1,1024]{1,0:T(1,128)} %bitcast.8, ...), custom_call_target="tpu_custom_call" | custom-call | tf_op jit(solution)/shard_map/fused/pallas_call | solution.py:766
  76.8 2.9 %emit.1 = (bf16[384,1024]{1,0:T(8,128)(2,1)}, bf16[384,5120]{1,0:T(8,128)(2,1)}, f32[4,8,16,1024]{3,2,1,0:T(8,128)}, f32[40,128]{1,0:T(8,128)}, f32[8,128]{1,0:T(8,128)}) custom-call(bf16[384,1024]{1,0:T(8,128)(2,1)S(1)} %get-tuple-element.15.refs_0_, bf16[384,5120]{1,0:T(8,128)(2,1)S(1)} %get-tuple-element.16.refs_1_, ...), custom_call_target="tpu_custom_call" | custom-call | tf_op jit(solution)/shard_map/emit/pallas_call | solution.py:802

commit v6 on v5

--- a/solution.py
+++ b/solution.py
@@ -70,20 +70,34 @@
 
 class Wires:
     def __init__(self, send, recv, limit):
-        self.send, self.recv, self.limit, self.groups = send, recv, limit, []
-
-    def group(self, total):
-        i = len(self.groups)
+        self.send, self.recv, self.limit = send, recv, limit
+        self.count, self.lanes = 0, []
+
+    def lane(self, total):
+        self.lanes.append((self.send.at[len(self.lanes)], total))
+        return self.lanes[-1][0]
+
+    def group(self, total, lane=None):
+        i = self.count
+        self.count += 1
         assert i < self.limit, "sems"
-        self.groups.append(Group(self.send.at[i], self.recv.at[i], total))
-        return self.groups[-1]
-
-    def put(self, src, dst, device):
-        return self.group(dst).put(src, dst, device)
+        return Group(self.lane(total) if lane is None else lane, self.recv.at[i], total)
+
+    def put(self, src, dst, device, lane=None):
+        return self.group(dst, lane).put(src, dst, device)
 
     def drain(self):
-        for group in self.groups:
-            pltpu.make_async_copy(group.total, group.total, group.send).wait()
+        for sem, total in self.lanes:
+            pltpu.make_async_copy(total, total, sem).wait()
+
+
+def thirds(wires, ref):
+    blocks = pl.ds(0, HALF)
+    return [
+        wires.lane(ref.at[0, 0, pl.ds(0, 3), blocks]),
+        wires.lane(ref.at[0, pl.ds(0, 3), :, blocks]),
+        wires.lane(ref.at[pl.ds(0, 3), :, :, blocks]),
+    ]
 
 
 class Group:
@@ -131,7 +145,9 @@
         self.base = place.c * HALF
         self.stage = {}
         half = HALF // 2
-        self.pair = [wires.group(w.at[:, :, :, pl.ds(0, half)]) for _ in range(2)]
+        self.lanes = thirds(wires, w)
+        across = wires.lane(w.at[:, :, :, pl.ds(0, HALF)])
+        self.pair = [wires.group(w.at[:, :, :, pl.ds(0, half)], across) for _ in range(2)]
 
     def view(self, p, k, v, first, count):
         off, nb, h, order = PARTS[p]
@@ -141,7 +157,7 @@
 
     def move(self, group, p, k, v, first, count, device):
         ref = self.view(p, k, v, first, count)
-        group = group or self.wires.group(ref)
+        group = group or self.wires.group(ref, self.lanes[k])
         group.put(ref, ref, device)
         return group
 
@@ -150,7 +166,8 @@
         return first, h, n - h
 
     def start(self, p, k, batch=0, part=None):
-        place, axis, group = self.place, PARTS[p][3][k], self.wires.group
+        place, axis = self.place, PARTS[p][3][k]
+        group = functools.partial(self.wires.group, lane=self.lanes[k])
         first, lo, hi = self.span(p, k, batch)
         mid = first + lo
         me = place.pos[axis]
@@ -221,6 +238,7 @@
         self.place, self.wires, self.g, self.bufs = place, wires, g, bufs
         self.base = place.c * HALF
         self.stage = {}
+        self.lanes = thirds(wires, g)[::-1]
 
     def index(self, p, k, v, later):
         order = PARTS[p][3]
@@ -243,13 +261,14 @@
     def start(self, p, k, part=None):
         off, nb, h, order = PARTS[p]
         place, axis = self.place, order[k]
-        put, full = self.wires.put, (slice(None),) * (2 - k)
+        full = (slice(None),) * (2 - k)
+        put = functools.partial(self.wires.put, lane=self.lanes[k])
         up, down = place.ring(axis, 1), place.ring(axis, 3)
         over, under = place.at(axis, 1), place.at(axis, 3)
         across = place.at(axis, 2)
         ta, tb, fm, fp = self.bufs[p][k]
         if k == 2:
-            both = self.wires.group(self.g.at[0, 0, 0, pl.ds(0, 3 * nb)])
+            both = self.wires.group(self.g.at[0, 0, 0, pl.ds(0, 3 * nb)], self.lanes[k])
             both.put(self.view(p, k, across, 0, nb), ta, place.ring(axis, 2))
             both.put(self.view(p, k, over, 0, nb), fm, up)
             both.put(self.view(p, k, under, 0, nb), fp, down)
@@ -259,7 +278,7 @@
             a = put(self.view(p, k, across, 0, h), ta, up)
             b = put(self.view(p, k, across, h, nb - h), tb, down)
             lead = (pl.ds(0, 2), slice(None), slice(None)) if k == 0 else (0, pl.ds(0, 2), slice(None))
-            self.stage[p, k] = [a, b, self.wires.group(self.g.at[lead + (pl.ds(0, nb),)])]
+            self.stage[p, k] = [a, b, self.wires.group(self.g.at[lead + (pl.ds(0, nb),)], self.lanes[k])]
         if part != 0:
             rest = self.stage[p, k][2]
             rest.put(self.view(p, k, over, h, nb - h), fm.at[full + (pl.ds(h, nb - h),)], up)
@@ -434,12 +453,12 @@
         off, nb = PARTS[p][:2]
         _, at = plane(p, step)
         dst = half.at[at + (pl.ds(off, nb),)]
-        group = group or wires.group(dst)
+        group = group or wires.group(dst, swaps)
         group.put(g.at[at + (pl.ds(other + off, nb),)], dst, place.partner())
         return group
 
     def swap_rest(p):
-        group = wires.group(half.at[pl.ds(0, 3), :, :, pl.ds(0, PARTS[p][1])])
+        group = wires.group(half.at[pl.ds(0, 3), :, :, pl.ds(0, PARTS[p][1])], swaps)
         for step in (1, 3, 0):
             swap(p, step, group)
         return group
@@ -465,6 +484,7 @@
         merge(p, 1, 3, 0)
 
     far, near = [], []
+    swaps = wires.lane(half)
     gather = Gather(place, wires, w)
     scatter = Scatter(place, wires, g, scatter_bufs(flat))
     small = Small(place, wires, first, rest)
@@ -722,12 +742,10 @@
     forward(0, 0, 2)
     small_next(0)
     spread_on()
-    forward(0, 2, 3)
+    forward(0, 2, 4)
     spread_middle()
-    forward(0, 3, 4)
-    forward(1, 0, 1)
+    forward(1, 0, 2)
     small_next(1)
-    forward(1, 1, 2)
     spread_late()
     forward(1, 2, 4)
     small_next(2)
@@ -753,6 +771,7 @@
 
 
 SEMS = 81
+LANES = 24
 OUTS = (
     ((ROWS, KEYS), BF),
     ((ROWS, WIDTH), BF),
@@ -792,7 +811,7 @@
             pltpu.SMEM((40,), jnp.int32),
             pltpu.VMEM((1, WIDTH), F32),
             pltpu.VMEM((1, KEYS), F32),
-            pltpu.SemaphoreType.DMA((SEMS,)),
+            pltpu.SemaphoreType.DMA((LANES,)),
             pltpu.SemaphoreType.DMA((SEMS,)),
             pltpu.SemaphoreType.DMA((11,)),
         ] + scatter_scratch(),

time: 80 us -> 79.5 us (level)
  no operation moved by 1% of the time
where the time goes in v6:
time: 79.5 us; the launch traced here: 79.4 us
  Pallas kernels  78.6 us (99%)
  between operations  0.8 us (1%)
    pallas_call x1, Pallas kernels, fused(): pl.pallas_call(fused_kernel, out_shape=tuple((pltpu.VMEM(*out) for out in...  75.6 us
    pallas_call x1, Pallas kernels, fused(): pl.pallas_call(emit_kernel, out_shape=tuple((jax.ShapeDtypeStruct(*out) f...  2.92 us

profile of v6, /device:TPU:0, one launch (start us, length us, event | category | flops | bytes accessed | tf_op | source)
XLA Modules:
  0.0 79.4 jit_solution(9763802455705690937)
XLA Ops:
  0.6 75.6 %fused.1 = (bf16[384,1024]{1,0:T(8,128)(2,1)S(1)}, bf16[384,5120]{1,0:T(8,128)(2,1)S(1)}, f32[4,8,16,1024]{3,2,1,0:T(8,128)S(1)}, f32[40,128]{1,0:T(8,128)S(1)}, f32[8,128]{1,0:T(8,128)S(1)}) custom-call(s32[40]{0:T(128)} %slots_hbm.1, bf16[384,5120]{1,0:T(8,128)(2,1)} %tok_ref.1, f32[1,5120]{1,0:T(1,128)} %bitcast.7, f32[1,1024]{1,0:T(1,128)} %bitcast.8, ...), custom_call_target="tpu_custom_call" | custom-call | tf_op jit(solution)/shard_map/fused/pallas_call | solution.py:785
  76.3 2.9 %emit.1 = (bf16[384,1024]{1,0:T(8,128)(2,1)}, bf16[384,5120]{1,0:T(8,128)(2,1)}, f32[4,8,16,1024]{3,2,1,0:T(8,128)}, f32[40,128]{1,0:T(8,128)}, f32[8,128]{1,0:T(8,128)}) custom-call(bf16[384,1024]{1,0:T(8,128)(2,1)S(1)} %get-tuple-element.15.refs_0_, bf16[384,5120]{1,0:T(8,128)(2,1)S(1)} %get-tuple-element.16.refs_1_, ...), custom_call_target="tpu_custom_call" | custom-call | tf_op jit(solution)/shard_map/emit/pallas_call | solution.py:821

commit v7 on v6

--- a/solution.py
+++ b/solution.py
@@ -173,7 +173,9 @@
         me = place.pos[axis]
         up, down = place.ring(axis, 1), place.ring(axis, 3)
         if k == 0:
-            both = group(self.w.at[0, 0, 0, pl.ds(0, 3 * (lo + hi))])
+            if p == 0:
+                self.joint = group(self.w.at[0, 0, pl.ds(0, 3), pl.ds(0, HALF)])
+            both = self.joint
             for device in (place.ring(axis, 2), up, down):
                 self.move(both, p, k, me, 0, lo + hi, device)
             self.stage[p, k, 0] = both
@@ -218,7 +220,8 @@
         place, axis = self.place, order[k]
         first, lo, hi = self.span(p, k, batch)
         if k == 0:
-            self.stage[p, k, 0].wait()
+            if p == 0:
+                self.joint.wait()
             return
         self.stage[p, k, batch][3].wait()
         self.share(p, k, place.at(axis, 2), first, lo + hi, batch)
@@ -268,7 +271,9 @@
         across = place.at(axis, 2)
         ta, tb, fm, fp = self.bufs[p][k]
         if k == 2:
-            both = self.wires.group(self.g.at[0, 0, 0, pl.ds(0, 3 * nb)], self.lanes[k])
+            if p == 0:
+                self.joint = self.wires.group(self.g.at[0, 0, pl.ds(0, 3), pl.ds(0, HALF)], self.lanes[k])
+            both = self.joint
             both.put(self.view(p, k, across, 0, nb), ta, place.ring(axis, 2))
             both.put(self.view(p, k, over, 0, nb), fm, up)
             both.put(self.view(p, k, under, 0, nb), fp, down)
@@ -312,7 +317,8 @@
         ta, tb, fm, fp = self.bufs[p][k]
         g = self.g
         if k == 2:
-            self.stage[p, k].wait()
+            if p == 0:
+                self.joint.wait()
             idx = self.tile(p, k, me, (), 0, nb)
             total = (g[idx].astype(F32) + ta[...].astype(F32)) + (fm[...].astype(F32) + fp[...].astype(F32))
             g[idx] = total.astype(BF)
@@ -770,7 +776,7 @@
 LIMIT = 56 * 1024 * 1024
 
 
-SEMS = 81
+SEMS = 77
 LANES = 24
 OUTS = (
     ((ROWS, KEYS), BF),

time: 79.5 us -> 79.4 us (level)
  no operation moved by 1% of the time
where the time goes in v7:
time: 79.4 us; the launch traced here: 79.3 us
  Pallas kernels  78.5 us (99%)
  between operations  0.8 us (1%)
    pallas_call x1, Pallas kernels, fused(): pl.pallas_call(fused_kernel, out_shape=tuple((pltpu.VMEM(*out) for out in...  75.6 us
    pallas_call x1, Pallas kernels, fused(): pl.pallas_call(emit_kernel, out_shape=tuple((jax.ShapeDtypeStruct(*out) f...  2.92 us

profile of v7, /device:TPU:0, one launch (start us, length us, event | category | flops | bytes accessed | tf_op | source)
XLA Modules:
  0.0 79.3 jit_solution(12127404737213550033)
XLA Ops:
  0.6 75.6 %fused.1 = (bf16[384,1024]{1,0:T(8,128)(2,1)S(1)}, bf16[384,5120]{1,0:T(8,128)(2,1)S(1)}, f32[4,8,16,1024]{3,2,1,0:T(8,128)S(1)}, f32[40,128]{1,0:T(8,128)S(1)}, f32[8,128]{1,0:T(8,128)S(1)}) custom-call(s32[40]{0:T(128)} %slots_hbm.1, bf16[384,5120]{1,0:T(8,128)(2,1)} %tok_ref.1, f32[1,5120]{1,0:T(1,128)} %bitcast.7, f32[1,1024]{1,0:T(1,128)} %bitcast.8, ...), custom_call_target="tpu_custom_call" | custom-call | tf_op jit(solution)/shard_map/fused/pallas_call | solution.py:791
  76.2 2.9 %emit.1 = (bf16[384,1024]{1,0:T(8,128)(2,1)}, bf16[384,5120]{1,0:T(8,128)(2,1)}, f32[4,8,16,1024]{3,2,1,0:T(8,128)}, f32[40,128]{1,0:T(8,128)}, f32[8,128]{1,0:T(8,128)}) custom-call(bf16[384,1024]{1,0:T(8,128)(2,1)S(1)} %get-tuple-element.15.refs_0_, bf16[384,5120]{1,0:T(8,128)(2,1)S(1)} %get-tuple-element.16.refs_1_, ...), custom_call_target="tpu_custom_call" | custom-call | tf_op jit(solution)/shard_map/emit/pallas_call | solution.py:827
